TPU v7x, 256 devices: a whole 4x4x8 slice. The times are simulated.
256 devices in a mesh: dp: 16 (over x, y_hi, core), ctx: 16 (over y_lo, z).
Axes of the slice: x: 4, y: 4 (y_hi: 2, y_lo: 2; y = y_hi * 2 + y_lo), z: 8, core: 2. Of those that a mesh axis runs over, the one named last changes fastest.
Arguments:
- normed: bfloat16 [16, 2048, 5376], P('dp', 'ctx'), may hold values from -6 to 6
- queries: bfloat16 [16, 2048, 2048], P('dp', 'ctx'), may hold values from -8 to 8
- keys: bfloat16 [16, 2048, 1024], P('dp', 'ctx'), may hold values from -8 to 8
- values: bfloat16 [16, 2048, 1024], P('dp', 'ctx'), may hold values from -6 to 6
- out_grad: bfloat16 [16, 2048, 2048], P('dp', 'ctx'), may hold values from -150 to 150
- segment_ids: int32 [16, 2048], P('dp'), may hold values from 0 to 3, never falling along the last dimension, each value on 1 to 1536 neighbouring positions
Outputs:
- grad_queries: bfloat16 [16, 2048, 2048], P('dp', 'ctx')
- grad_keys: bfloat16 [16, 2048, 1024], P('dp', 'ctx')
- grad_values: bfloat16 [16, 2048, 1024], P('dp', 'ctx')
- grad_weight: bfloat16 [5376, 1024], P('ctx', 'dp')
Inputs may be any that keep to these rules, and one draw needn't show every extreme that they name: `segment_ids`: within a sequence the document numbers never fall, and a document has at most 1536 positions.
All inputs are finite; a program needn't handle non-finite values.
Results may differ from a plain program's by a relative error of at most 0.022.
Values may be sent and summed in bfloat16 or wider, within the bound.
No kernel may reach another device: no remote copies, remote signals or barrier semaphores. Data moves between devices by JAX's collectives and lax.ppermute only.
A program may use at most 128 MiB of HBM per device.

v0:
```python
import functools
import math

import jax
import jax.numpy as jnp
from jax import lax
from jax.experimental import pallas as pl
from jax.experimental.pallas import tpu as pltpu
from jax.sharding import Mesh, PartitionSpec as P


HEAD = 128
WINDOW = 1024
QUERY_SCALAR = 168.0
BF = jnp.bfloat16
F32 = jnp.float32
RING = 8
HOPS = (0, 4, 3, -3, 2, -2, 1, -1)
PARTS = ((0, 4), (4, 8))


VMEM = pl.BlockSpec(memory_space=pltpu.VMEM)
SMEM = pl.BlockSpec(memory_space=pltpu.SMEM)


def call(kernel, outs, n_in, scratch=(), flops=1_000_000):
    return pl.pallas_call(
        kernel,
        out_shape=outs,
        in_specs=[SMEM] + [VMEM] * n_in,
        out_specs=jax.tree.map(lambda _: VMEM, outs),
        scratch_shapes=list(scratch),
        cost_estimate=pl.CostEstimate(flops=flops, bytes_accessed=2_000_000, transcendentals=0),
        compiler_params=pltpu.CompilerParams(vmem_limit_bytes=60_000_000),
    )


def shape(*dims, dtype=BF):
    return jax.ShapeDtypeStruct(dims, dtype)


def rotate(x, by):
    return lax.ppermute(x, "z", [(i, (i + by) % RING) for i in range(RING)])


def nt(a, b):
    return lax.dot_general(a, b, (((1,), (1,)), ((), ())), preferred_element_type=F32)


def nn(a, b):
    return lax.dot_general(a, b, (((1,), (0,)), ((), ())), preferred_element_type=F32)


def heads_kernel(z_ref, k, v, kv):
    for head in range(RING):
        kv[head, :, :HEAD] = k[:, head * HEAD : (head + 1) * HEAD]
        kv[head, :, HEAD:] = v[:, head * HEAD : (head + 1) * HEAD]


def pack_kernel(z_ref, q, g, *outs):
    z = z_ref[0]
    for n, hop in enumerate(HOPS):
        head = lax.rem(z + hop + RING, RING)
        wide = pl.ds(pl.multiple_of(head * 2 * HEAD, 2 * HEAD), 2 * HEAD)
        outs[n][:, : 2 * HEAD] = q[:, wide]
        outs[n][:, 2 * HEAD :] = g[:, wide]


def in_order(z, pieces, out):
    rows = pieces[0].shape[0]
    for ref, hop in zip(pieces, HOPS):
        source = lax.rem(z - hop + RING, RING)
        out[pl.ds(pl.multiple_of(source * rows, rows), rows), :] = ref[...]


def turn_kernel(z_ref, ids, x, out, lo_ref):
    _, features = x.shape
    part = out.shape[2]
    for b in range(features // 128):
        t = x[:, 128 * b : 128 * b + 128].T
        at = 128 * b
        while at < 128 * b + 128:
            owner = at // part
            stop = min(128 * b + 128, (owner + 1) * part)
            lo = at - owner * part
            out[owner % RING, owner // RING, lo : lo + stop - at, :] = t[at - 128 * b : stop - 128 * b]
            at = stop
    yl = z_ref[2]
    every = ids[...]
    own = ids[pl.ds(pl.multiple_of(yl * RING, RING), RING), :]
    doc = jnp.zeros(own.shape, jnp.int32)
    for d in range(1, 4):
        doc = jnp.where(own >= d, jnp.sum((every < d).astype(jnp.int32)), doc)
    block = lax.broadcasted_iota(jnp.int32, own.shape, 0)
    at = lax.broadcasted_iota(jnp.int32, own.shape, 1)
    lo = jnp.maximum(doc - (yl * (RING * 128) - WINDOW + block * 128), at + 1)
    lo_ref[:, :128] = lo
    lo_ref[:, 128:] = lo


def scores(kw, q, lo, scale):
    s = nt(kw, q)
    key = lax.broadcasted_iota(jnp.int32, s.shape, 0)
    row = lax.broadcasted_iota(jnp.int32, (1, s.shape[1]), 1)
    last = jnp.where(row >= 128, row - 128, row) + WINDOW
    ok = (key >= lo) & (key <= last)
    return jnp.where(ok, s * scale, -jnp.inf)


def stacked(qg, block, first):
    rows = pl.ds(pl.multiple_of(block * 128, 128), 128)
    return jnp.concatenate([qg[rows, first : first + 128], qg[rows, first + 128 : first + 256]], axis=0)


def first_kernel(scale, z_ref, lo_ref, *refs):
    pieces, (kv_own, kv_prev), (dv_prev, dv_own, stats, qg) = refs[:8], refs[8:10], refs[10:14]
    acc, keys = refs[14:]
    in_order(z_ref[0], pieces, qg)
    acc[...] = jnp.zeros_like(acc)
    keys[:WINDOW, :] = kv_prev[:, :HEAD]
    keys[WINDOW:, :] = kv_own[:, :HEAD]

    def step(i, carry):
        span = pl.ds(pl.multiple_of(i * 128, 128), WINDOW + 128)
        lo = lo_ref[pl.ds(i, 1), :]
        s = scores(keys[span, :], stacked(qg, i, 0), lo, scale)
        top = jnp.max(s, axis=0, keepdims=True)
        e = jnp.exp2(s - top)
        inverse = 1.0 / jnp.sum(e, axis=0, keepdims=True)
        stats[pl.ds(i, 1), :] = top
        stats[pl.ds(8 + i, 1), :] = inverse
        low = (e * inverse).astype(BF)
        acc[span, :] += nn(low, stacked(qg, i, 256))
        return carry

    lax.fori_loop(0, 8, step, 0, unroll=True)
    dv_prev[...] = acc[:WINDOW, :].astype(BF)
    dv_own[...] = acc[WINDOW:, :]


def second_kernel(scale, softmax_scale, lower, upper, z_ref, lo_ref, qg, stats, kv_own, kv_prev, *refs):
    acc, dq = refs[1:3] if lower else refs[:2]
    dk_prev, keys, vals, turned = refs[-4:]
    acc[...] = refs[0][...] if lower else jnp.zeros_like(acc)
    begin, end = 128 * lower, 128 * upper
    keys[begin:WINDOW, :] = kv_prev[begin:, :HEAD]
    keys[WINDOW : WINDOW + end, :] = kv_own[:end, :HEAD]
    vals[begin:WINDOW, :] = kv_prev[begin:, HEAD:]
    vals[WINDOW : WINDOW + end, :] = kv_own[:end, HEAD:]
    for b in range(lower, upper + 8):
        turned[:, 128 * b : 128 * b + 128] = keys[128 * b : 128 * b + 128, :].T

    def step(i, carry):
        at = pl.multiple_of(i * 128, 128)
        span = pl.ds(at, WINDOW + 128)
        lo = lo_ref[pl.ds(i, 1), :]
        q = stacked(qg, i, 0)
        s = scores(keys[span, :], q, lo, scale)
        full = jnp.exp2(s - stats[pl.ds(i, 1), :]) * stats[pl.ds(8 + i, 1), :]
        gp = nt(vals[span, :], stacked(qg, i, 256))
        delta = jnp.sum(full.astype(BF).astype(F32) * gp, axis=0, keepdims=True)
        ds = (full * (gp - delta)).astype(BF)
        acc[span, :] += nn(ds, q)
        back = nn(turned[:, span], ds) * softmax_scale
        dq[i - lower, :, :HEAD] = back[:, :128].T.astype(BF)
        dq[i - lower, :, HEAD:] = back[:, 128:].T.astype(BF)
        return carry

    lax.fori_loop(lower, upper, step, 0, unroll=True)
    if upper == RING:
        dk_prev[...] = (acc[:WINDOW, :] * softmax_scale).astype(BF)


def back_kernel(softmax_scale, z_ref, low, high, acc, got, *outs):
    z = z_ref[0]
    split = low.shape[0]
    for n, hop in enumerate(HOPS):
        block = lax.rem(z + hop + RING, RING)
        rows = pl.ds(pl.multiple_of(block * HEAD, HEAD), HEAD)
        upper = pl.ds(pl.multiple_of(WINDOW + block * HEAD, HEAD), HEAD)

        @pl.when(block < split)
        def _():
            outs[n][:, : 2 * HEAD] = low[jnp.minimum(block, split - 1)]

        @pl.when(block >= split)
        def _():
            outs[n][:, : 2 * HEAD] = high[jnp.maximum(block - split, 0)]

        outs[n][:, 2 * HEAD :] = (acc[upper, :] * softmax_scale + got[rows, :].astype(F32)).astype(BF)


def unpack_kernel(z_ref, *refs):
    z = z_ref[0]
    dq, dk = refs[-2:]
    for ref, hop in zip(refs[:-2], HOPS):
        head = lax.rem(z - hop + RING, RING)
        dq[:, pl.ds(pl.multiple_of(head * 2 * HEAD, 2 * HEAD), 2 * HEAD)] = ref[:, : 2 * HEAD]
        dk[:, pl.ds(pl.multiple_of(head * HEAD, HEAD), HEAD)] = ref[:, 2 * HEAD :]


def halves(w, core, part):
    lane = lax.broadcasted_iota(jnp.int32, (part // 2, 128), 1) < 64
    swapped = pltpu.roll(w, 64, 1)
    near = jnp.where(core == 0, w, swapped)
    far = jnp.where(core == 0, swapped, w)
    out = []
    for row in range(2):
        a, b = row * part, row * part + part // 2
        c = b + part // 2
        out.append((jnp.where(lane, near[a:b], far[b:c]), jnp.where(lane, far[a:b], near[b:c]).astype(BF)))
    return out


def weight_kernel(hops, z_ref, features, *refs):
    n = len(hops)
    blocks, (gv, mine, other, lhs) = refs[:n], refs[n:]
    z = z_ref[0]
    part = features.shape[2]
    for source in range(RING):
        for row in range(2):
            lhs[row * part : (row + 1) * part, 128 * source : 128 * source + 128] = features[source, row]
    own = pl.ds(pl.multiple_of(z * 128, 128), 128)
    for ref, hop in zip(blocks, hops):
        head = lax.rem(z - hop + RING, RING)
        gv[:, pl.ds(pl.multiple_of(head * HEAD, HEAD), HEAD)] = ref[own, :]
        for row, (a, b) in enumerate(halves(nn(lhs[...], ref[...]), z_ref[1], part)):
            mine[head, row] = a
            other[head, row] = b


def last_weight_kernel(z_ref, lhs, block, mine, other):
    part = lhs.shape[0] // 2
    for row, (a, b) in enumerate(halves(nn(lhs[...], block[...]), z_ref[1], part)):
        mine[row] = a
        other[row] = b


def join_kernel(z_ref, both, last, got, out, total, sem):
    total[...] = (last[...] + got[...].astype(F32)).astype(BF)
    copy = pltpu.make_async_copy(total, out.at[lax.rem(z_ref[0] + 4, RING)], sem)
    copy.start()
    copy.wait()


def body(normed, queries, keys, values, out_grad, segment_ids):
    z = lax.axis_index("z")
    yl = lax.axis_index("yl")
    core = lax.axis_index("core")
    place = jnp.stack([z, core, yl]).astype(jnp.int32)
    softmax_scale = QUERY_SCALAR ** (-0.5)
    scale = softmax_scale * math.log2(math.e)
    count = queries.shape[1]
    features = normed.shape[2]
    part = features // 16
    half = part // 2
    row = RING * count

    packed = call(heads_kernel, shape(RING, count, 2 * HEAD), 2)(place, keys[0], values[0])
    kv_own = lax.all_to_all(packed, "z", 0, 0, tiled=True).reshape(row, 2 * HEAD)
    packed = call(pack_kernel, [shape(count, 4 * HEAD)] * 8, 2)(place, queries[0], out_grad[0])
    qg = [packed[0]]
    for n in range(1, 8):
        qg.append(rotate(packed[n], HOPS[n]))
    turned, lo = call(
        turn_kernel, [shape(RING, 2, part, count), shape(RING, 256, dtype=jnp.int32)], 2
    )(place, segment_ids.reshape(2 * RING, count), normed[0])
    kv_prev = lax.ppermute(kv_own, "yl", [(0, 1)])
    spread = lax.all_to_all(turned, "z", 0, 0, tiled=True)

    dv_prev, dv_own, stats, rows = call(
        functools.partial(first_kernel, scale),
        [shape(row, HEAD), shape(row, HEAD, dtype=F32), shape(16, 256, dtype=F32), shape(row, 4 * HEAD)],
        11,
        [pltpu.VMEM((2 * row, HEAD), F32), pltpu.VMEM((2 * row, HEAD), BF)],
        flops=2_000_000_000,
    )(place, lo, *qg, kv_own, kv_prev)

    got = lax.ppermute(dv_prev, "yl", [(1, 0)])
    dv = (dv_own + got.astype(F32)).astype(BF)
    blocks = {0: dv}
    for s in range(1, 5):
        blocks[s] = rotate(blocks[s - 1], 1)
        if s < 4:
            blocks[-s] = rotate(blocks[1 - s], -1)

    acc = None
    dq = []
    for n, (lower, upper) in enumerate(PARTS):
        outs = [shape(2 * row, HEAD, dtype=F32), shape(upper - lower, count, 2 * HEAD), shape(row, HEAD)]
        acc, piece, dk_prev = call(
            functools.partial(second_kernel, scale, softmax_scale, lower, upper),
            outs,
            5 + (n > 0),
            [pltpu.VMEM((2 * row, HEAD), BF), pltpu.VMEM((2 * row, HEAD), BF), pltpu.VMEM((HEAD, 2 * row), BF)],
            flops=1_500_000_000,
        )(place, lo, rows, stats, kv_own, kv_prev, *([acc] if n else []))
        dq.append(piece)
    got = lax.ppermute(dk_prev, "yl", [(1, 0)])
    back = call(functools.partial(back_kernel, softmax_scale), [shape(count, 3 * HEAD)] * 8, 4)(place, *dq, acc, got)
    home = [back[0]]
    for n in range(1, 8):
        home.append(rotate(back[n], HOPS[n]))
    grad_queries, grad_keys = call(
        unpack_kernel, [shape(count, 2 * RING * HEAD), shape(count, RING * HEAD)], 8
    )(place, *home)

    early = [h for h in HOPS if h != 4]
    gv, mine, other, lhs = call(
        functools.partial(weight_kernel, early),
        [
            shape(count, RING * HEAD),
            shape(RING, 2, half, HEAD, dtype=F32),
            shape(RING, 2, half, HEAD),
            shape(2 * part, row),
        ],
        8,
        flops=2_000_000_000,
    )(place, spread, *[blocks[h] for h in early])
    got = lax.ppermute(other, "core", [(0, 1), (1, 0)])
    both = (mine + got.astype(F32)).astype(BF)
    last, other = call(
        last_weight_kernel, [shape(2, half, HEAD, dtype=F32), shape(2, half, HEAD)], 2, flops=300_000_000
    )(place, lhs, blocks[4])
    got = lax.ppermute(other, "core", [(0, 1), (1, 0)])
    both = pl.pallas_call(
        join_kernel,
        out_shape=shape(RING, 2, half, HEAD),
        in_specs=[SMEM, pl.BlockSpec(memory_space=pl.ANY), VMEM, VMEM],
        out_specs=pl.BlockSpec(memory_space=pl.ANY),
        scratch_shapes=[pltpu.VMEM((2, half, HEAD), BF), pltpu.SemaphoreType.DMA],
        input_output_aliases={1: 0},
        name="join",
    )(place, both, last, got)
    arrived = lax.all_to_all(both.reshape(2 * RING, half, HEAD), ("x", "yh", "yl"), 0, 0, tiled=True)
    total = arrived.astype(F32).sum(axis=0) * (row * 2 * 16) ** (-0.5)
    grad_weight = jnp.concatenate([total[:, :64], total[:, 64:]], axis=0).astype(BF)
    far = lax.dynamic_slice_in_dim(blocks[4], z * count, count, 0)
    gv = lax.dynamic_update_slice_in_dim(gv, far, lax.rem(z + 4, RING) * HEAD, 1)
    return grad_queries[None], grad_keys[None], gv[None], grad_weight


def solution(mesh):
    fine = Mesh(mesh.devices.reshape(4, 2, 2, 2, RING), ("x", "yh", "core", "yl", "z"))
    dp, ctx = ("x", "yh", "core"), ("yl", "z")

    return jax.shard_map(
        body,
        mesh=fine,
        in_specs=(P(dp, ctx, None),) * 5 + (P(dp, None),),
        out_specs=(P(dp, ctx, None),) * 3 + (P(ctx, dp),),
        check_vma=False,
    )
```

profile of v0, /device:TPU:2, one launch (start us, length us, event | category | flops | bytes accessed | tf_op | source)
XLA Modules:
  0.0 213.5 jit_solution(5368760195759730253)
XLA Ops:
  0.6 0.7 pad_add_fusion.z_ref
  1.3 1.9 shard_map.95
  3.2 8.5 %all-to-all-start = ((bf16[8,128,256]{2,1,0:T(8,128)(2,1)}), bf16[8,128,256]{2,1,0:T(8,128)(2,1)S(1)}, u32[]{:S(2)}, u32[]{:S(2)}) async-start(bf16[8,128,256]{2,1,0:T(8,128)(2,1)} %shard_map.95), calls=%async_computation | async-start | bytes 1048576 | tf_op jit(solution)/shard_map/all_to_all | solution.py:260
  11.7 2.9 %shard_map.93 = (bf16[8,2,336,128]{3,2,1,0:T(8,128)(2,1)}, s32[8,256]{1,0:T(8,128)}) custom-call(s32[3]{0:T(128)} %pad_add_fusion.z_ref, s32[16,128]{1,0:T(8,128)} %bitcast.26, bf16[128,5376]{1,0:T(8,128)(2,1)} %bitcast.17), custom_call_target="tpu_custom_call" | custom-call | flops 1000000 | bytes 2000000 | tf_op jit(solution)/shard_map/pallas_call | solution.py:265
  14.6 14.6 %all-to-all-done = bf16[8,128,256]{2,1,0:T(8,128)(2,1)S(1)} async-done(((bf16[8,128,256]{2,1,0:T(8,128)(2,1)}), bf16[8,128,256]{2,1,0:T(8,128)(2,1)S(1)}, u32[]{:S(2)}, u32[]{:S(2)}) %all-to-all-start) | async-done | bytes 524320 | tf_op jit(solution)/shard_map/all_to_all | solution.py:260
  29.2 3.6 %all-to-all-start.1 = ((bf16[8,2,336,128]{3,2,1,0:T(8,128)(2,1)}), bf16[8,2,336,128]{3,2,1,0:T(8,128)(2,1)S(1)}, u32[]{:S(2)}, u32[]{:S(2)}) async-start(bf16[8,2,336,128]{3,2,1,0:T(8,128)(2,1)} %get-tuple-element.65), calls=%async_computation.1 | async-start | bytes 2752512 | tf_op jit(solution)/shard_map/all_to_all | solution.py:269
  32.8 3.5 %collective-permute-start.7 = (bf16[1024,256]{1,0:T(8,128)(2,1)S(1)}, bf16[1024,256]{1,0:T(8,128)(2,1)S(1)}, u32[]{:S(2)}, u32[]{:S(2)}) collective-permute-start(bf16[1024,256]{1,0:T(8,128)(2,1)S(1)} %bitcast.18), channel_id=1, source_target_pairs={{0,8},{1,9},{2,10},{3,11},{4,12},{5,13},{6,14},{7,15},{16,24},{17,... | collective-permute-start | bytes 1572872 | tf_op jit(solution)/shard_map/ppermute | solution.py:268
  36.3 2.3 %shard_map.94 = (bf16[128,512]{1,0:T(8,128)(2,1)}, bf16[128,512]{1,0:T(8,128)(2,1)}, bf16[128,512]{1,0:T(8,128)(2,1)}, bf16[128,512]{1,0:T(8,128)(2,1)}, bf16[12...) custom-call(s32[3]{0:T(128)} %pad_add_fusion.z_ref, ...), custom_call_target="tpu_custom_call" | custom-call | flops 1000000 | bytes 2000000 | tf_op jit(solution)/shard_map/pallas_call | solution.py:261
  38.6 5.8 %collective-permute-start = (bf16[128,512]{1,0:T(8,128)(2,1)}, bf16[128,512]{1,0:T(8,128)(2,1)S(1)}, u32[]{:S(2)}, u32[]{:S(2)}) collective-permute-start(bf16[128,512]{1,0:T(8,128)(2,1)} %get-tuple-element.41), channel_id=1, source_target_pairs={{0,4},{1,5},{2,6},{3,7},{4,0},{5,1},{6,2},{7,3},{8,12},{9,13},{10,... | collective-permute-start | bytes 393224 | tf_op jit(solution)/shard_map/ppermute | solution.py:43
  44.4 0.6 collective-permute-start.1
  45.0 4.5 %collective-permute-start.2 = (bf16[128,512]{1,0:T(8,128)(2,1)}, bf16[128,512]{1,0:T(8,128)(2,1)S(1)}, u32[]{:S(2)}, u32[]{:S(2)}) collective-permute-start(bf16[128,512]{1,0:T(8,128)(2,1)} %get-tuple-element.43), channel_id=1, source_target_pairs={{0,5},{1,6},{2,7},{3,0},{4,1},{5,2},{6,3},{7,4},{8,13},{9,14},{10,... | collective-permute-start | bytes 393224 | tf_op jit(solution)/shard_map/ppermute | solution.py:43
  49.5 0.6 collective-permute-start.3
  50.0 27.4 %collective-permute-done.refs_1_ = bf16[128,512]{1,0:T(8,128)(2,1)S(1)} collective-permute-done((bf16[128,512]{1,0:T(8,128)(2,1)}, bf16[128,512]{1,0:T(8,128)(2,1)S(1)}, u32[]{:S(2)}, u32[]{:S(2)}) %collective-permute-start) | collective-permute-done | bytes 131104 | tf_op jit(solution)/shard_map/ppermute | solution.py:43
  77.4 4.6 %collective-permute-done.1.refs_2_ = bf16[128,512]{1,0:T(8,128)(2,1)S(1)} collective-permute-done((bf16[128,512]{1,0:T(8,128)(2,1)}, bf16[128,512]{1,0:T(8,128)(2,1)S(1)}, u32[]{:S(2)}, u32[]{:S(2)}) %collective-permute-start.1) | collective-permute-done | bytes 131104 | tf_op jit(solution)/shard_map/ppermute | solution.py:43
  82.1 2.7 %collective-permute-start.5 = (bf16[128,512]{1,0:T(8,128)(2,1)}, bf16[128,512]{1,0:T(8,128)(2,1)S(1)}, u32[]{:S(2)}, u32[]{:S(2)}) collective-permute-start(bf16[128,512]{1,0:T(8,128)(2,1)} %get-tuple-element.46), channel_id=1, source_target_pairs={{0,1},{1,2},{2,3},{3,4},{4,5},{5,6},{6,7},{7,0},{8,9},{9,10},{10,1... | collective-permute-start | bytes 393224 | tf_op jit(solution)/shard_map/ppermute | solution.py:43
  84.8 0.5 collective-permute-start.6
  85.4 1.2 collective-permute-done.4.refs_5_
  86.6 2.1 collective-permute-done.5.refs_6_
  88.7 1.3 collective-permute-done.6.refs_7_
  90.1 0.6 copy-done.27
  90.7 0.2 copy-done.14
  90.8 6.6 %shard_map.96 = (bf16[1024,128]{1,0:T(8,128)(2,1)}, f32[1024,128]{1,0:T(8,128)}, f32[16,256]{1,0:T(8,128)}, bf16[1024,512]{1,0:T(8,128)(2,1)}) custom-call(s32[3]{0:T(128)} %pad_add_fusion.z_ref, s32[8,256]{1,0:T(8,128)} %get-tuple-element.39.lo_ref, bf16[128,512]{1,0:T(8,128)(2,1)} %get-tuple-element.40.refs_0_, bf16[128,512]{1,0:T(8,128)(2,1)} %copy-done.21, ...), custom_call_target="tpu_custom_call" | custom-call | flops 2000000000 | bytes 2000000 | tf_op jit(solution)/shard_map/pallas_call | solution.py:271
  97.5 1.3 collective-permute-start.16
  98.8 7.2 %collective-permute-done.16 = bf16[1024,128]{1,0:T(8,128)(2,1)S(1)} collective-permute-done((bf16[1024,128]{1,0:T(8,128)(2,1)}, bf16[1024,128]{1,0:T(8,128)(2,1)S(1)}, u32[]{:S(2)}, u32[]{:S(2)}) %collective-permute-start.16) | collective-permute-done | bytes 262176 | tf_op jit(solution)/shard_map/ppermute | solution.py:279
  105.9 1.1 add_convert_fusion.1.refs_0_
  107.1 0.9 collective-permute-start.17
  108.0 2.4 %collective-permute-start.20 = (bf16[1024,128]{1,0:T(8,128)(2,1)S(1)}, bf16[1024,128]{1,0:T(8,128)(2,1)S(1)}, u32[]{:S(2)}, u32[]{:S(2)}) collective-permute-start(bf16[1024,128]{1,0:T(8,128)(2,1)S(1)} %add_convert_fusion.1.refs_0_), channel_id=1, source_target_pairs={{0,7},{1,0},{2,1},{3,2},{4,3},{5,4},{6,5},{7,6},{8,15},{9,8},{10,9... | collective-permute-start | bytes 786440 | tf_op jit(solution)/shard_map/ppermute | solution.py:43
  110.4 5.2 %collective-permute-done.17.refs_5_ = bf16[1024,128]{1,0:T(8,128)(2,1)S(1)} collective-permute-done((bf16[1024,128]{1,0:T(8,128)(2,1)S(1)}, bf16[1024,128]{1,0:T(8,128)(2,1)S(1)}, u32[]{:S(2)}, u32[]{:S(2)}) %collective-permute-start.17) | collective-permute-done | bytes 262176 | tf_op jit(solution)/shard_map/ppermute | solution.py:43
  115.6 3.5 %collective-permute-start.21 = (bf16[1024,128]{1,0:T(8,128)(2,1)S(1)}, bf16[1024,128]{1,0:T(8,128)(2,1)S(1)}, u32[]{:S(2)}, u32[]{:S(2)}) collective-permute-start(bf16[1024,128]{1,0:T(8,128)(2,1)S(1)} %collective-permute-done.20.refs_6_), channel_id=1, source_target_pairs={{0,7},{1,0},{2,1},{3,2},{4,3},{5,4},{6,5},{7,6},{8,15},{9,8},{10,9... | collective-permute-start | bytes 786440 | tf_op jit(solution)/shard_map/ppermute | solution.py:43
  119.1 6.1 %collective-permute-done.18.refs_3_ = bf16[1024,128]{1,0:T(8,128)(2,1)S(1)} collective-permute-done((bf16[1024,128]{1,0:T(8,128)(2,1)S(1)}, bf16[1024,128]{1,0:T(8,128)(2,1)S(1)}, u32[]{:S(2)}, u32[]{:S(2)}) %collective-permute-start.18) | collective-permute-done | bytes 262176 | tf_op jit(solution)/shard_map/ppermute | solution.py:43
  125.2 3.7 %collective-permute-start.22 = (bf16[1024,128]{1,0:T(8,128)(2,1)S(1)}, bf16[1024,128]{1,0:T(8,128)(2,1)S(1)}, u32[]{:S(2)}, u32[]{:S(2)}) collective-permute-start(bf16[1024,128]{1,0:T(8,128)(2,1)S(1)} %collective-permute-done.21.refs_4_), channel_id=1, source_target_pairs={{0,7},{1,0},{2,1},{3,2},{4,3},{5,4},{6,5},{7,6},{8,15},{9,8},{10,9... | collective-permute-start | bytes 786440 | tf_op jit(solution)/shard_map/ppermute | solution.py:43
  128.9 3.8 %collective-permute-done.19.refs_1_ = bf16[1024,128]{1,0:T(8,128)(2,1)S(1)} collective-permute-done((bf16[1024,128]{1,0:T(8,128)(2,1)S(1)}, bf16[1024,128]{1,0:T(8,128)(2,1)S(1)}, u32[]{:S(2)}, u32[]{:S(2)}) %collective-permute-start.19) | collective-permute-done | bytes 262176 | tf_op jit(solution)/shard_map/ppermute | solution.py:43
  132.9 0.6 copy-done.17
  133.4 0.7 copy-done.20
  134.1 6.5 %shard_map.101 = (bf16[128,1024]{1,0:T(8,128)(2,1)}, f32[8,2,168,128]{3,2,1,0:T(8,128)}, bf16[8,2,168,128]{3,2,1,0:T(8,128)(2,1)}, bf16[672,1024]{1,0:T(8,128)(2,1)}) custom-call(s32[3]{0:T(128)} %pad_add_fusion.z_ref, bf16[8,2,336,128]{3,2,1,0:T(8,128)(2,1)} %copy-done, bf16[1024,128]{1,0:T(8,128)(2,1)} %copy-done.4, bf16[1024,128]{1,0:T(8,128)(2,1)} %copy-done.17, ...), custom_call_target="tpu_custom_call" | custom-call | flops 2000000000 | bytes 2000000 | tf_op jit(solution)/shard_map/pallas_call | solution.py:309
  140.7 6.8 %shard_map.97 = (f32[2048,128]{1,0:T(8,128)}, bf16[4,128,256]{2,1,0:T(8,128)(2,1)}, bf16[1024,128]{1,0:T(8,128)(2,1)}) custom-call(s32[3]{0:T(128)} %pad_add_fusion.z_ref, s32[8,256]{1,0:T(8,128)} %get-tuple-element.39.lo_ref, bf16[1024,512]{1,0:T(8,128)(2,1)} %get-tuple-element.48.qg, f32[16,256]{1,0:T(8,128)} %get-tuple-element.49.stats, ...), custom_call_target="tpu_custom_call" | custom-call | flops 1500000000 | bytes 2000000 | tf_op jit(solution)/shard_map/pallas_call | solution.py:291
  147.6 3.4 %collective-permute-done.23.block = bf16[1024,128]{1,0:T(8,128)(2,1)S(1)} collective-permute-done((bf16[1024,128]{1,0:T(8,128)(2,1)}, bf16[1024,128]{1,0:T(8,128)(2,1)S(1)}, u32[]{:S(2)}, u32[]{:S(2)}) %collective-permute-start.23) | collective-permute-done | bytes 262176 | tf_op jit(solution)/shard_map/ppermute | solution.py:43
  151.0 0.7 copy-done.3
  151.7 2.7 %shard_map.102 = (f32[2,168,128]{2,1,0:T(8,128)}, bf16[2,168,128]{2,1,0:T(8,128)(2,1)}) custom-call(s32[3]{0:T(128)} %pad_add_fusion.z_ref, bf16[672,1024]{1,0:T(8,128)(2,1)} %get-tuple-element.71.lhs, bf16[1024,128]{1,0:T(8,128)(2,1)} %copy-done.3), custom_call_target="tpu_custom_call" | custom-call | flops 300000000 | bytes 2000000 | tf_op jit(solution)/shard_map/pallas_call | solution.py:322
  154.3 1.0 add_convert_fusion.both
  155.3 0.5 collective-permute-done.25.got
  155.8 0.6 copy-done.13
  156.4 1.6 join.1
  158.1 7.5 %all-to-all-start.2 = ((bf16[16,168,128]{2,1,0:T(8,128)(2,1)}), bf16[16,168,128]{2,1,0:T(8,128)(2,1)S(1)}, u32[]{:S(2)}, u32[]{:S(2)}) async-start(bf16[16,168,128]{2,1,0:T(8,128)(2,1)} %bitcast.16), calls=%async_computation.2 | async-start | bytes 1376256 | tf_op jit(solution)/shard_map/all_to_all | solution.py:335
  165.6 7.1 %shard_map.98 = (f32[2048,128]{1,0:T(8,128)}, bf16[4,128,256]{2,1,0:T(8,128)(2,1)}, bf16[1024,128]{1,0:T(8,128)(2,1)}) custom-call(s32[3]{0:T(128)} %pad_add_fusion.z_ref, s32[8,256]{1,0:T(8,128)} %get-tuple-element.39.lo_ref, bf16[1024,512]{1,0:T(8,128)(2,1)} %get-tuple-element.48.qg, f32[16,256]{1,0:T(8,128)} %get-tuple-element.49.stats, ...), custom_call_target="tpu_custom_call" | custom-call | flops 1500000000 | bytes 2000000 | tf_op jit(solution)/shard_map/pallas_call | solution.py:291
  172.7 1.3 collective-permute-start.8
  174.0 8.6 %collective-permute-done.8.got = bf16[1024,128]{1,0:T(8,128)(2,1)S(1)} collective-permute-done((bf16[1024,128]{1,0:T(8,128)(2,1)}, bf16[1024,128]{1,0:T(8,128)(2,1)S(1)}, u32[]{:S(2)}, u32[]{:S(2)}) %collective-permute-start.8) | collective-permute-done | bytes 262176 | tf_op jit(solution)/shard_map/ppermute | solution.py:299
  182.6 0.7 copy-done.5
  183.3 2.5 %shard_map.99 = (bf16[128,384]{1,0:T(8,128)(2,1)}, bf16[128,384]{1,0:T(8,128)(2,1)}, bf16[128,384]{1,0:T(8,128)(2,1)}, bf16[128,384]{1,0:T(8,128)(2,1)}, bf16[12...) custom-call(s32[3]{0:T(128)} %pad_add_fusion.z_ref, ...), custom_call_target="tpu_custom_call" | custom-call | flops 1000000 | bytes 2000000 | tf_op jit(solution)/shard_map/pallas_call | solution.py:300
  185.8 2.0 collective-permute-start.9
  187.8 3.0 %collective-permute-start.10 = (bf16[128,384]{1,0:T(8,128)(2,1)}, bf16[128,384]{1,0:T(8,128)(2,1)S(1)}, u32[]{:S(2)}, u32[]{:S(2)}) collective-permute-start(bf16[128,384]{1,0:T(8,128)(2,1)} %get-tuple-element.57), channel_id=1, source_target_pairs={{0,3},{1,4},{2,5},{3,6},{4,7},{5,0},{6,1},{7,2},{8,11},{9,12},{10,... | collective-permute-start | bytes 294920 | tf_op jit(solution)/shard_map/ppermute | solution.py:43
  190.9 2.0 collective-permute-start.11
  192.8 1.6 collective-permute-start.12
  194.4 2.6 %collective-permute-start.13 = (bf16[128,384]{1,0:T(8,128)(2,1)}, bf16[128,384]{1,0:T(8,128)(2,1)S(1)}, u32[]{:S(2)}, u32[]{:S(2)}) collective-permute-start(bf16[128,384]{1,0:T(8,128)(2,1)} %get-tuple-element.60), channel_id=1, source_target_pairs={{0,6},{1,7},{2,0},{3,1},{4,2},{5,3},{6,4},{7,5},{8,14},{9,15},{10,... | collective-permute-start | bytes 294920 | tf_op jit(solution)/shard_map/ppermute | solution.py:43
  197.0 2.4 %collective-permute-done.9.refs_1_ = bf16[128,384]{1,0:T(8,128)(2,1)S(1)} collective-permute-done((bf16[128,384]{1,0:T(8,128)(2,1)}, bf16[128,384]{1,0:T(8,128)(2,1)S(1)}, u32[]{:S(2)}, u32[]{:S(2)}) %collective-permute-start.9) | collective-permute-done | bytes 98336 | tf_op jit(solution)/shard_map/ppermute | solution.py:43
  199.3 4.1 %collective-permute-done.10.refs_2_ = bf16[128,384]{1,0:T(8,128)(2,1)S(1)} collective-permute-done((bf16[128,384]{1,0:T(8,128)(2,1)}, bf16[128,384]{1,0:T(8,128)(2,1)S(1)}, u32[]{:S(2)}, u32[]{:S(2)}) %collective-permute-start.10) | collective-permute-done | bytes 98336 | tf_op jit(solution)/shard_map/ppermute | solution.py:43
  203.5 0.7 collective-permute-start.15
  204.2 1.1 collective-permute-done.13.refs_5_
  205.3 0.2 collective-permute-done.14.refs_6_
  205.5 2.8 %collective-permute-done.15.refs_7_ = bf16[128,384]{1,0:T(8,128)(2,1)S(1)} collective-permute-done((bf16[128,384]{1,0:T(8,128)(2,1)}, bf16[128,384]{1,0:T(8,128)(2,1)S(1)}, u32[]{:S(2)}, u32[]{:S(2)}) %collective-permute-start.15) | collective-permute-done | bytes 98336 | tf_op jit(solution)/shard_map/ppermute | solution.py:43
  208.4 0.6 copy-done.12
  209.0 2.3 %shard_map.100 = (bf16[128,2048]{1,0:T(8,128)(2,1)}, bf16[128,1024]{1,0:T(8,128)(2,1)}) custom-call(s32[3]{0:T(128)} %pad_add_fusion.z_ref, bf16[128,384]{1,0:T(8,128)(2,1)} %get-tuple-element.55.refs_0_, bf16[128,384]{1,0:T(8,128)(2,1)} %copy-done.6, bf16[128,384]{1,0:T(8,128)(2,1)} %copy-done.7, bf16[128,384]{1,0:T(8,128)(2,1)} %copy-done.8, ...), custom_call_target="tpu_custom_call" | custom-call | flops 1000000 | bytes 2000000 | tf_op jit(solution)/shard_map/pallas_call | solution.py:304
  211.2 1.4 bitcast_dynamic-update-slice_fusion
  212.8 0.7 copy.11
  (70 shorter events, 0.7 us)
Async XLA Ops:
  3.2 26.0 %all-to-all-start = ((bf16[8,128,256]{2,1,0:T(8,128)(2,1)}), bf16[8,128,256]{2,1,0:T(8,128)(2,1)S(1)}, u32[]{:S(2)}, u32[]{:S(2)}) async-start(bf16[8,128,256]{2,1,0:T(8,128)(2,1)} %shard_map.95), calls=%async_computation | async-start | bytes 1048576 | tf_op jit(solution)/shard_map/all_to_all | solution.py:260
  29.2 3.6 %copy-start.2 = (bf16[8,128,256]{2,1,0:T(8,128)(2,1)}, bf16[8,128,256]{2,1,0:T(8,128)(2,1)S(1)}, u32[]{:S(2)}) copy-start(bf16[8,128,256]{2,1,0:T(8,128)(2,1)S(1)} %all-to-all-done) | copy-start | bytes 1572868
  29.2 99.8 %all-to-all-start.1 = ((bf16[8,2,336,128]{3,2,1,0:T(8,128)(2,1)}), bf16[8,2,336,128]{3,2,1,0:T(8,128)(2,1)S(1)}, u32[]{:S(2)}, u32[]{:S(2)}) async-start(bf16[8,2,336,128]{3,2,1,0:T(8,128)(2,1)} %get-tuple-element.65), calls=%async_computation.1 | async-start | bytes 2752512 | tf_op jit(solution)/shard_map/all_to_all | solution.py:269
  32.8 57.2 %collective-permute-start.7 = (bf16[1024,256]{1,0:T(8,128)(2,1)S(1)}, bf16[1024,256]{1,0:T(8,128)(2,1)S(1)}, u32[]{:S(2)}, u32[]{:S(2)}) collective-permute-start(bf16[1024,256]{1,0:T(8,128)(2,1)S(1)} %bitcast.18), channel_id=1, source_target_pairs={{0,8},{1,9},{2,10},{3,11},{4,12},{5,13},{6,14},{7,15},{16,24},{17,... | collective-permute-start | bytes 1572872 | tf_op jit(solution)/shard_map/ppermute | solution.py:268
  38.6 38.8 %collective-permute-start = (bf16[128,512]{1,0:T(8,128)(2,1)}, bf16[128,512]{1,0:T(8,128)(2,1)S(1)}, u32[]{:S(2)}, u32[]{:S(2)}) collective-permute-start(bf16[128,512]{1,0:T(8,128)(2,1)} %get-tuple-element.41), channel_id=1, source_target_pairs={{0,4},{1,5},{2,6},{3,7},{4,0},{5,1},{6,2},{7,3},{8,12},{9,13},{10,... | collective-permute-start | bytes 393224 | tf_op jit(solution)/shard_map/ppermute | solution.py:43
  44.4 37.6 %collective-permute-start.1 = (bf16[128,512]{1,0:T(8,128)(2,1)}, bf16[128,512]{1,0:T(8,128)(2,1)S(1)}, u32[]{:S(2)}, u32[]{:S(2)}) collective-permute-start(bf16[128,512]{1,0:T(8,128)(2,1)} %get-tuple-element.42), channel_id=1, source_target_pairs={{0,3},{1,4},{2,5},{3,6},{4,7},{5,0},{6,1},{7,2},{8,11},{9,12},{10,... | collective-permute-start | bytes 393224 | tf_op jit(solution)/shard_map/ppermute | solution.py:43
  45.0 39.8 %collective-permute-start.2 = (bf16[128,512]{1,0:T(8,128)(2,1)}, bf16[128,512]{1,0:T(8,128)(2,1)S(1)}, u32[]{:S(2)}, u32[]{:S(2)}) collective-permute-start(bf16[128,512]{1,0:T(8,128)(2,1)} %get-tuple-element.43), channel_id=1, source_target_pairs={{0,5},{1,6},{2,7},{3,0},{4,1},{5,2},{6,3},{7,4},{8,13},{9,14},{10,... | collective-permute-start | bytes 393224 | tf_op jit(solution)/shard_map/ppermute | solution.py:43
  49.5 36.0 %collective-permute-start.3 = (bf16[128,512]{1,0:T(8,128)(2,1)}, bf16[128,512]{1,0:T(8,128)(2,1)S(1)}, u32[]{:S(2)}, u32[]{:S(2)}) collective-permute-start(bf16[128,512]{1,0:T(8,128)(2,1)} %get-tuple-element.44), channel_id=1, source_target_pairs={{0,2},{1,3},{2,4},{3,5},{4,6},{5,7},{6,0},{7,1},{8,10},{9,11},{10,... | collective-permute-start | bytes 393224 | tf_op jit(solution)/shard_map/ppermute | solution.py:43
  77.4 12.6 %copy-start.21 = (bf16[128,512]{1,0:T(8,128)(2,1)}, bf16[128,512]{1,0:T(8,128)(2,1)S(1)}, u32[]{:S(2)}) copy-start(bf16[128,512]{1,0:T(8,128)(2,1)S(1)} %collective-permute-done.refs_1_) | copy-start | bytes 393220
  77.4 9.2 %collective-permute-start.4 = (bf16[128,512]{1,0:T(8,128)(2,1)}, bf16[128,512]{1,0:T(8,128)(2,1)S(1)}, u32[]{:S(2)}, u32[]{:S(2)}) collective-permute-start(bf16[128,512]{1,0:T(8,128)(2,1)} %get-tuple-element.45), channel_id=1, source_target_pairs={{0,6},{1,7},{2,0},{3,1},{4,2},{5,3},{6,4},{7,5},{8,14},{9,15},{10,... | collective-permute-start | bytes 393224 | tf_op jit(solution)/shard_map/ppermute | solution.py:43
  82.1 7.9 %copy-start.22 = (bf16[128,512]{1,0:T(8,128)(2,1)}, bf16[128,512]{1,0:T(8,128)(2,1)S(1)}, u32[]{:S(2)}) copy-start(bf16[128,512]{1,0:T(8,128)(2,1)S(1)} %collective-permute-done.1.refs_2_) | copy-start | bytes 393220
  82.1 6.6 %collective-permute-start.5 = (bf16[128,512]{1,0:T(8,128)(2,1)}, bf16[128,512]{1,0:T(8,128)(2,1)S(1)}, u32[]{:S(2)}, u32[]{:S(2)}) collective-permute-start(bf16[128,512]{1,0:T(8,128)(2,1)} %get-tuple-element.46), channel_id=1, source_target_pairs={{0,1},{1,2},{2,3},{3,4},{4,5},{5,6},{6,7},{7,0},{8,9},{9,10},{10,1... | collective-permute-start | bytes 393224 | tf_op jit(solution)/shard_map/ppermute | solution.py:43
  84.8 5.2 %copy-start.23 = (bf16[128,512]{1,0:T(8,128)(2,1)}, bf16[128,512]{1,0:T(8,128)(2,1)S(1)}, u32[]{:S(2)}) copy-start(bf16[128,512]{1,0:T(8,128)(2,1)S(1)} %collective-permute-done.2.refs_3_) | copy-start | bytes 393220
  84.8 5.2 %collective-permute-start.6 = (bf16[128,512]{1,0:T(8,128)(2,1)}, bf16[128,512]{1,0:T(8,128)(2,1)S(1)}, u32[]{:S(2)}, u32[]{:S(2)}) collective-permute-start(bf16[128,512]{1,0:T(8,128)(2,1)} %get-tuple-element.47), channel_id=1, source_target_pairs={{0,7},{1,0},{2,1},{3,2},{4,3},{5,4},{6,5},{7,6},{8,15},{9,8},{10,9... | collective-permute-start | bytes 393224 | tf_op jit(solution)/shard_map/ppermute | solution.py:43
  85.4 4.6 %copy-start.24 = (bf16[128,512]{1,0:T(8,128)(2,1)}, bf16[128,512]{1,0:T(8,128)(2,1)S(1)}, u32[]{:S(2)}) copy-start(bf16[128,512]{1,0:T(8,128)(2,1)S(1)} %collective-permute-done.3.refs_4_) | copy-start | bytes 393220
  86.6 3.4 %copy-start.25 = (bf16[128,512]{1,0:T(8,128)(2,1)}, bf16[128,512]{1,0:T(8,128)(2,1)S(1)}, u32[]{:S(2)}) copy-start(bf16[128,512]{1,0:T(8,128)(2,1)S(1)} %collective-permute-done.4.refs_5_) | copy-start | bytes 393220
  88.7 1.4 copy-start.26
  90.0 0.6 copy-start.27
  90.0 0.8 copy-start.14
  97.5 8.5 %collective-permute-start.16 = (bf16[1024,128]{1,0:T(8,128)(2,1)}, bf16[1024,128]{1,0:T(8,128)(2,1)S(1)}, u32[]{:S(2)}, u32[]{:S(2)}) collective-permute-start(bf16[1024,128]{1,0:T(8,128)(2,1)} %get-tuple-element.67), channel_id=1, source_target_pairs={{8,0},{9,1},{10,2},{11,3},{12,4},{13,5},{14,6},{15,7},{24,16},{25,... | collective-permute-start | bytes 786440 | tf_op jit(solution)/shard_map/ppermute | solution.py:279
  107.0 25.8 %copy-start.4 = (bf16[1024,128]{1,0:T(8,128)(2,1)}, bf16[1024,128]{1,0:T(8,128)(2,1)S(1)}, u32[]{:S(2)}) copy-start(bf16[1024,128]{1,0:T(8,128)(2,1)S(1)} %add_convert_fusion.1.refs_0_) | copy-start | bytes 786436
  107.1 8.5 %collective-permute-start.17 = (bf16[1024,128]{1,0:T(8,128)(2,1)S(1)}, bf16[1024,128]{1,0:T(8,128)(2,1)S(1)}, u32[]{:S(2)}, u32[]{:S(2)}) collective-permute-start(bf16[1024,128]{1,0:T(8,128)(2,1)S(1)} %add_convert_fusion.1.refs_0_), channel_id=1, source_target_pairs={{0,1},{1,2},{2,3},{3,4},{4,5},{5,6},{6,7},{7,0},{8,9},{9,10},{10,1... | collective-permute-start | bytes 786440 | tf_op jit(solution)/shard_map/ppermute | solution.py:43
  108.0 7.6 %collective-permute-start.20 = (bf16[1024,128]{1,0:T(8,128)(2,1)S(1)}, bf16[1024,128]{1,0:T(8,128)(2,1)S(1)}, u32[]{:S(2)}, u32[]{:S(2)}) collective-permute-start(bf16[1024,128]{1,0:T(8,128)(2,1)S(1)} %add_convert_fusion.1.refs_0_), channel_id=1, source_target_pairs={{0,7},{1,0},{2,1},{3,2},{4,3},{5,4},{6,5},{7,6},{8,15},{9,8},{10,9... | collective-permute-start | bytes 786440 | tf_op jit(solution)/shard_map/ppermute | solution.py:43
  115.6 17.3 %copy-start.15 = (bf16[1024,128]{1,0:T(8,128)(2,1)}, bf16[1024,128]{1,0:T(8,128)(2,1)S(1)}, u32[]{:S(2)}) copy-start(bf16[1024,128]{1,0:T(8,128)(2,1)S(1)} %collective-permute-done.17.refs_5_) | copy-start | bytes 786436
  115.6 9.6 %collective-permute-start.18 = (bf16[1024,128]{1,0:T(8,128)(2,1)S(1)}, bf16[1024,128]{1,0:T(8,128)(2,1)S(1)}, u32[]{:S(2)}, u32[]{:S(2)}) collective-permute-start(bf16[1024,128]{1,0:T(8,128)(2,1)S(1)} %collective-permute-done.17.refs_5_), channel_id=1, source_target_pairs={{0,1},{1,2},{2,3},{3,4},{4,5},{5,6},{6,7},{7,0},{8,9},{9,10},{10,1... | collective-permute-start | bytes 786440 | tf_op jit(solution)/shard_map/ppermute | solution.py:43
  115.6 17.3 %copy-start.16 = (bf16[1024,128]{1,0:T(8,128)(2,1)}, bf16[1024,128]{1,0:T(8,128)(2,1)S(1)}, u32[]{:S(2)}) copy-start(bf16[1024,128]{1,0:T(8,128)(2,1)S(1)} %collective-permute-done.20.refs_6_) | copy-start | bytes 786436
  115.6 9.7 %collective-permute-start.21 = (bf16[1024,128]{1,0:T(8,128)(2,1)S(1)}, bf16[1024,128]{1,0:T(8,128)(2,1)S(1)}, u32[]{:S(2)}, u32[]{:S(2)}) collective-permute-start(bf16[1024,128]{1,0:T(8,128)(2,1)S(1)} %collective-permute-done.20.refs_6_), channel_id=1, source_target_pairs={{0,7},{1,0},{2,1},{3,2},{4,3},{5,4},{6,5},{7,6},{8,15},{9,8},{10,9... | collective-permute-start | bytes 786440 | tf_op jit(solution)/shard_map/ppermute | solution.py:43
  125.2 7.7 %copy-start.18 = (bf16[1024,128]{1,0:T(8,128)(2,1)}, bf16[1024,128]{1,0:T(8,128)(2,1)S(1)}, u32[]{:S(2)}) copy-start(bf16[1024,128]{1,0:T(8,128)(2,1)S(1)} %collective-permute-done.18.refs_3_) | copy-start | bytes 786436
  125.2 7.6 %collective-permute-start.19 = (bf16[1024,128]{1,0:T(8,128)(2,1)S(1)}, bf16[1024,128]{1,0:T(8,128)(2,1)S(1)}, u32[]{:S(2)}, u32[]{:S(2)}) collective-permute-start(bf16[1024,128]{1,0:T(8,128)(2,1)S(1)} %collective-permute-done.18.refs_3_), channel_id=1, source_target_pairs={{0,1},{1,2},{2,3},{3,4},{4,5},{5,6},{6,7},{7,0},{8,9},{9,10},{10,1... | collective-permute-start | bytes 786440 | tf_op jit(solution)/shard_map/ppermute | solution.py:43
  125.2 7.6 %copy-start.19 = (bf16[1024,128]{1,0:T(8,128)(2,1)}, bf16[1024,128]{1,0:T(8,128)(2,1)S(1)}, u32[]{:S(2)}) copy-start(bf16[1024,128]{1,0:T(8,128)(2,1)S(1)} %collective-permute-done.21.refs_4_) | copy-start | bytes 786436
  125.2 7.6 %collective-permute-start.22 = (bf16[1024,128]{1,0:T(8,128)(2,1)S(1)}, bf16[1024,128]{1,0:T(8,128)(2,1)S(1)}, u32[]{:S(2)}, u32[]{:S(2)}) collective-permute-start(bf16[1024,128]{1,0:T(8,128)(2,1)S(1)} %collective-permute-done.21.refs_4_), channel_id=1, source_target_pairs={{0,7},{1,0},{2,1},{3,2},{4,3},{5,4},{6,5},{7,6},{8,15},{9,8},{10,9... | collective-permute-start | bytes 786440 | tf_op jit(solution)/shard_map/ppermute | solution.py:43
  128.9 3.9 %copy-start = (bf16[8,2,336,128]{3,2,1,0:T(8,128)(2,1)}, bf16[8,2,336,128]{3,2,1,0:T(8,128)(2,1)S(1)}, u32[]{:S(2)}) copy-start(bf16[8,2,336,128]{3,2,1,0:T(8,128)(2,1)S(1)} %all-to-all-done.1.features) | copy-start | bytes 4128772
  132.7 0.7 copy-start.17
  133.4 0.7 copy-start.20
  140.6 13.7 %collective-permute-start.24 = (bf16[8,2,168,128]{3,2,1,0:T(8,128)(2,1)}, bf16[8,2,168,128]{3,2,1,0:T(8,128)(2,1)S(1)}, u32[]{:S(2)}, u32[]{:S(2)}) collective-permute-start(bf16[8,2,168,128]{3,2,1,0:T(8,128)(2,1)} %get-tuple-element.70), channel_id=1, source_target_pairs={{0,16},{16,0},{1,17},{17,1},{2,18},{18,2},{3,19},{19,3},{4,20},{20... | collective-permute-start | bytes 2064392 | tf_op jit(solution)/shard_map/ppermute | solution.py:320
  140.6 10.3 %collective-permute-start.23 = (bf16[1024,128]{1,0:T(8,128)(2,1)}, bf16[1024,128]{1,0:T(8,128)(2,1)S(1)}, u32[]{:S(2)}, u32[]{:S(2)}) collective-permute-start(bf16[1024,128]{1,0:T(8,128)(2,1)} %copy-done.17), channel_id=1, source_target_pairs={{0,1},{1,2},{2,3},{3,4},{4,5},{5,6},{6,7},{7,0},{8,9},{9,10},{10,1... | collective-permute-start | bytes 786440 | tf_op jit(solution)/shard_map/ppermute | solution.py:43
  147.6 6.8 %copy-start.1 = (f32[8,2,168,128]{3,2,1,0:T(8,128)S(1)}, f32[8,2,168,128]{3,2,1,0:T(8,128)}, u32[]{:S(2)}) copy-start(f32[8,2,168,128]{3,2,1,0:T(8,128)} %get-tuple-element.69) | copy-start | bytes 4128772
  151.0 0.7 copy-start.3
  154.3 1.5 collective-permute-start.25
  155.8 0.6 copy-start.13
  158.1 54.5 %all-to-all-start.2 = ((bf16[16,168,128]{2,1,0:T(8,128)(2,1)}), bf16[16,168,128]{2,1,0:T(8,128)(2,1)S(1)}, u32[]{:S(2)}, u32[]{:S(2)}) async-start(bf16[16,168,128]{2,1,0:T(8,128)(2,1)} %bitcast.16), calls=%async_computation.2 | async-start | bytes 1376256 | tf_op jit(solution)/shard_map/all_to_all | solution.py:335
  172.7 9.9 %collective-permute-start.8 = (bf16[1024,128]{1,0:T(8,128)(2,1)}, bf16[1024,128]{1,0:T(8,128)(2,1)S(1)}, u32[]{:S(2)}, u32[]{:S(2)}) collective-permute-start(bf16[1024,128]{1,0:T(8,128)(2,1)} %get-tuple-element.54), channel_id=1, source_target_pairs={{8,0},{9,1},{10,2},{11,3},{12,4},{13,5},{14,6},{15,7},{24,16},{25,... | collective-permute-start | bytes 786440 | tf_op jit(solution)/shard_map/ppermute | solution.py:299
  182.6 0.7 copy-start.5
  185.8 13.5 %collective-permute-start.9 = (bf16[128,384]{1,0:T(8,128)(2,1)}, bf16[128,384]{1,0:T(8,128)(2,1)S(1)}, u32[]{:S(2)}, u32[]{:S(2)}) collective-permute-start(bf16[128,384]{1,0:T(8,128)(2,1)} %get-tuple-element.56), channel_id=1, source_target_pairs={{0,4},{1,5},{2,6},{3,7},{4,0},{5,1},{6,2},{7,3},{8,12},{9,13},{10,... | collective-permute-start | bytes 294920 | tf_op jit(solution)/shard_map/ppermute | solution.py:43
  187.8 15.7 %collective-permute-start.10 = (bf16[128,384]{1,0:T(8,128)(2,1)}, bf16[128,384]{1,0:T(8,128)(2,1)S(1)}, u32[]{:S(2)}, u32[]{:S(2)}) collective-permute-start(bf16[128,384]{1,0:T(8,128)(2,1)} %get-tuple-element.57), channel_id=1, source_target_pairs={{0,3},{1,4},{2,5},{3,6},{4,7},{5,0},{6,1},{7,2},{8,11},{9,12},{10,... | collective-permute-start | bytes 294920 | tf_op jit(solution)/shard_map/ppermute | solution.py:43
  190.9 13.4 %collective-permute-start.11 = (bf16[128,384]{1,0:T(8,128)(2,1)}, bf16[128,384]{1,0:T(8,128)(2,1)S(1)}, u32[]{:S(2)}, u32[]{:S(2)}) collective-permute-start(bf16[128,384]{1,0:T(8,128)(2,1)} %get-tuple-element.58), channel_id=1, source_target_pairs={{0,5},{1,6},{2,7},{3,0},{4,1},{5,2},{6,3},{7,4},{8,13},{9,14},{10,... | collective-permute-start | bytes 294920 | tf_op jit(solution)/shard_map/ppermute | solution.py:43
  192.8 11.4 %collective-permute-start.12 = (bf16[128,384]{1,0:T(8,128)(2,1)}, bf16[128,384]{1,0:T(8,128)(2,1)S(1)}, u32[]{:S(2)}, u32[]{:S(2)}) collective-permute-start(bf16[128,384]{1,0:T(8,128)(2,1)} %get-tuple-element.59), channel_id=1, source_target_pairs={{0,2},{1,3},{2,4},{3,5},{4,6},{5,7},{6,0},{7,1},{8,10},{9,11},{10,... | collective-permute-start | bytes 294920 | tf_op jit(solution)/shard_map/ppermute | solution.py:43
  194.4 10.9 %collective-permute-start.13 = (bf16[128,384]{1,0:T(8,128)(2,1)}, bf16[128,384]{1,0:T(8,128)(2,1)S(1)}, u32[]{:S(2)}, u32[]{:S(2)}) collective-permute-start(bf16[128,384]{1,0:T(8,128)(2,1)} %get-tuple-element.60), channel_id=1, source_target_pairs={{0,6},{1,7},{2,0},{3,1},{4,2},{5,3},{6,4},{7,5},{8,14},{9,15},{10,... | collective-permute-start | bytes 294920 | tf_op jit(solution)/shard_map/ppermute | solution.py:43
  199.3 9.0 %copy-start.6 = (bf16[128,384]{1,0:T(8,128)(2,1)}, bf16[128,384]{1,0:T(8,128)(2,1)S(1)}, u32[]{:S(2)}) copy-start(bf16[128,384]{1,0:T(8,128)(2,1)S(1)} %collective-permute-done.9.refs_1_) | copy-start | bytes 294916
  199.3 6.1 %collective-permute-start.14 = (bf16[128,384]{1,0:T(8,128)(2,1)}, bf16[128,384]{1,0:T(8,128)(2,1)S(1)}, u32[]{:S(2)}, u32[]{:S(2)}) collective-permute-start(bf16[128,384]{1,0:T(8,128)(2,1)} %get-tuple-element.61), channel_id=1, source_target_pairs={{0,1},{1,2},{2,3},{3,4},{4,5},{5,6},{6,7},{7,0},{8,9},{9,10},{10,1... | collective-permute-start | bytes 294920 | tf_op jit(solution)/shard_map/ppermute | solution.py:43
  203.5 4.8 %copy-start.7 = (bf16[128,384]{1,0:T(8,128)(2,1)}, bf16[128,384]{1,0:T(8,128)(2,1)S(1)}, u32[]{:S(2)}) copy-start(bf16[128,384]{1,0:T(8,128)(2,1)S(1)} %collective-permute-done.10.refs_2_) | copy-start | bytes 294916
  203.5 4.8 %collective-permute-start.15 = (bf16[128,384]{1,0:T(8,128)(2,1)}, bf16[128,384]{1,0:T(8,128)(2,1)S(1)}, u32[]{:S(2)}, u32[]{:S(2)}) collective-permute-start(bf16[128,384]{1,0:T(8,128)(2,1)} %get-tuple-element.62), channel_id=1, source_target_pairs={{0,7},{1,0},{2,1},{3,2},{4,3},{5,4},{6,5},{7,6},{8,15},{9,8},{10,9... | collective-permute-start | bytes 294920 | tf_op jit(solution)/shard_map/ppermute | solution.py:43
  204.2 4.1 %copy-start.8 = (bf16[128,384]{1,0:T(8,128)(2,1)}, bf16[128,384]{1,0:T(8,128)(2,1)S(1)}, u32[]{:S(2)}) copy-start(bf16[128,384]{1,0:T(8,128)(2,1)S(1)} %collective-permute-done.11.refs_3_) | copy-start | bytes 294916
  204.2 4.1 %copy-start.9 = (bf16[128,384]{1,0:T(8,128)(2,1)}, bf16[128,384]{1,0:T(8,128)(2,1)S(1)}, u32[]{:S(2)}) copy-start(bf16[128,384]{1,0:T(8,128)(2,1)S(1)} %collective-permute-done.12.refs_4_) | copy-start | bytes 294916
  205.3 3.0 %copy-start.10 = (bf16[128,384]{1,0:T(8,128)(2,1)}, bf16[128,384]{1,0:T(8,128)(2,1)S(1)}, u32[]{:S(2)}) copy-start(bf16[128,384]{1,0:T(8,128)(2,1)S(1)} %collective-permute-done.13.refs_5_) | copy-start | bytes 294916
  205.5 2.9 %copy-start.11 = (bf16[128,384]{1,0:T(8,128)(2,1)}, bf16[128,384]{1,0:T(8,128)(2,1)S(1)}, u32[]{:S(2)}) copy-start(bf16[128,384]{1,0:T(8,128)(2,1)S(1)} %collective-permute-done.14.refs_6_) | copy-start | bytes 294916
  208.3 0.6 copy-start.12
where the time goes:
time: 214 us
  waiting for transfers between devices  96.8 us (45%)
  starting transfers between devices  62.7 us (29%)
  Pallas kernels  43.3 us (20%)
  local copies, waits for them, and re-layouts  6.92 us (3%)
  other arithmetic  2.88 us (1%)
    ppermute x21, waiting for transfers between devices, rotate(): return lax.ppermute(x, 'z', [(i, (i + by) % RING) for i in range(RING)])  66 us
    ppermute x21, starting transfers between devices, rotate(): return lax.ppermute(x, 'z', [(i, (i + by) % RING) for i in range(RING)])  37.1 us
    all_to_all x1, waiting for transfers between devices, body(): lax.all_to_all(packed, 'z', 0, 0, tiled=True).reshape(row, 2 * HEAD)  14.6 us
    pallas_call x2, Pallas kernels, body(): call(functools.partial(second_kernel, scale, softmax_scale, lower, upper)...  14 us
    ppermute x1, waiting for transfers between devices, body(): got = lax.ppermute(dk_prev, 'yl', [(1, 0)])  8.62 us
    all_to_all x1, starting transfers between devices, body(): lax.all_to_all(packed, 'z', 0, 0, tiled=True).reshape(row, 2 * HEAD)  8.47 us
    all_to_all x1, starting transfers between devices, body(): lax.all_to_all(both.reshape(2 * RING, half, HEAD), ('x', 'yh', 'yl'), 0,...  7.49 us
    ppermute x1, waiting for transfers between devices, body(): got = lax.ppermute(dv_prev, 'yl', [(1, 0)])  7.18 us
  transfers between devices with their start and end apart: 29, of which 21 were waited for; matrix products, arithmetic and copies ran while one was open for 2% of the time, Pallas kernels for 16%

commit v1 on v0

--- a/solution.py
+++ b/solution.py
@@ -17,21 +17,27 @@
 RING = 8
 HOPS = (0, 4, 3, -3, 2, -2, 1, -1)
 PARTS = ((0, 4), (4, 8))
+GROUPS = ((0, 1, -1), (2, -2), (3, -3), (4,))
+SOON = (4, 3, -3)
+LATE = (0, 2, -2, 1, -1)
+LIMIT = 4_000_000
+LARGE = 10_000_000
 
 
 VMEM = pl.BlockSpec(memory_space=pltpu.VMEM)
+ANY = pl.BlockSpec(memory_space=pl.ANY)
 SMEM = pl.BlockSpec(memory_space=pltpu.SMEM)
 
 
-def call(kernel, outs, n_in, scratch=(), flops=1_000_000):
+def call(kernel, outs, n_in, scratch=(), flops=1_000_000, limit=LIMIT, loose=(), loose_out=False):
     return pl.pallas_call(
         kernel,
         out_shape=outs,
-        in_specs=[SMEM] + [VMEM] * n_in,
-        out_specs=jax.tree.map(lambda _: VMEM, outs),
+        in_specs=[SMEM] + [ANY if n in loose else VMEM for n in range(n_in)],
+        out_specs=jax.tree.map(lambda _: ANY if loose_out else VMEM, outs),
         scratch_shapes=list(scratch),
         cost_estimate=pl.CostEstimate(flops=flops, bytes_accessed=2_000_000, transcendentals=0),
-        compiler_params=pltpu.CompilerParams(vmem_limit_bytes=60_000_000),
+        compiler_params=pltpu.CompilerParams(vmem_limit_bytes=limit),
     )
 
 
@@ -51,10 +57,16 @@
     return lax.dot_general(a, b, (((1,), (0,)), ((), ())), preferred_element_type=F32)
 
 
-def heads_kernel(z_ref, k, v, kv):
+def heads_kernel(k, v, kv, sem):
+    copies = []
     for head in range(RING):
-        kv[head, :, :HEAD] = k[:, head * HEAD : (head + 1) * HEAD]
-        kv[head, :, HEAD:] = v[:, head * HEAD : (head + 1) * HEAD]
+        columns = pl.ds(head * HEAD, HEAD)
+        copies.append(pltpu.make_async_copy(k.at[:, columns], kv.at[head, :, pl.ds(0, HEAD)], sem.at[head]))
+        copies.append(pltpu.make_async_copy(v.at[:, columns], kv.at[head, :, pl.ds(HEAD, HEAD)], sem.at[RING + head]))
+    for copy in copies:
+        copy.start()
+    for copy in copies:
+        copy.wait()
 
 
 def pack_kernel(z_ref, q, g, *outs):
@@ -66,11 +78,15 @@
         outs[n][:, 2 * HEAD :] = g[:, wide]
 
 
-def in_order(z, pieces, out):
+def in_order(z, pieces, out, sem):
     rows = pieces[0].shape[0]
-    for ref, hop in zip(pieces, HOPS):
+    copies = []
+    for n, (ref, hop) in enumerate(zip(pieces, HOPS)):
         source = lax.rem(z - hop + RING, RING)
-        out[pl.ds(pl.multiple_of(source * rows, rows), rows), :] = ref[...]
+        at = out.at[pl.ds(pl.multiple_of(source * rows, rows), rows), :]
+        copies.append(pltpu.make_async_copy(ref, at, sem.at[n]))
+        copies[-1].start()
+    return copies
 
 
 def turn_kernel(z_ref, ids, x, out, lo_ref):
@@ -114,11 +130,13 @@
 
 def first_kernel(scale, z_ref, lo_ref, *refs):
     pieces, (kv_own, kv_prev), (dv_prev, dv_own, stats, qg) = refs[:8], refs[8:10], refs[10:14]
-    acc, keys = refs[14:]
-    in_order(z_ref[0], pieces, qg)
+    acc, keys, sem = refs[14:]
+    copies = in_order(z_ref[0], pieces, qg, sem)
     acc[...] = jnp.zeros_like(acc)
     keys[:WINDOW, :] = kv_prev[:, :HEAD]
     keys[WINDOW:, :] = kv_own[:, :HEAD]
+    for copy in copies:
+        copy.wait()
 
     def step(i, carry):
         span = pl.ds(pl.multiple_of(i * 128, 128), WINDOW + 128)
@@ -166,37 +184,44 @@
         dq[i - lower, :, HEAD:] = back[:, 128:].T.astype(BF)
         return carry
 
-    lax.fori_loop(lower, upper, step, 0, unroll=True)
+    lax.fori_loop(lower, upper, step, 0, unroll=2)
     if upper == RING:
         dk_prev[...] = (acc[:WINDOW, :] * softmax_scale).astype(BF)
 
 
-def back_kernel(softmax_scale, z_ref, low, high, acc, got, *outs):
+def back_kernel(softmax_scale, hops, z_ref, low, high, acc, got, *outs):
     z = z_ref[0]
     split = low.shape[0]
-    for n, hop in enumerate(HOPS):
+    for out, hop in zip(outs, hops):
         block = lax.rem(z + hop + RING, RING)
         rows = pl.ds(pl.multiple_of(block * HEAD, HEAD), HEAD)
         upper = pl.ds(pl.multiple_of(WINDOW + block * HEAD, HEAD), HEAD)
 
         @pl.when(block < split)
         def _():
-            outs[n][:, : 2 * HEAD] = low[jnp.minimum(block, split - 1)]
+            out[:, : 2 * HEAD] = low[jnp.minimum(block, split - 1)]
 
         @pl.when(block >= split)
         def _():
-            outs[n][:, : 2 * HEAD] = high[jnp.maximum(block - split, 0)]
-
-        outs[n][:, 2 * HEAD :] = (acc[upper, :] * softmax_scale + got[rows, :].astype(F32)).astype(BF)
+            out[:, : 2 * HEAD] = high[jnp.maximum(block - split, 0)]
+
+        out[:, 2 * HEAD :] = (acc[upper, :] * softmax_scale + got[rows, :].astype(F32)).astype(BF)
 
 
 def unpack_kernel(z_ref, *refs):
     z = z_ref[0]
-    dq, dk = refs[-2:]
-    for ref, hop in zip(refs[:-2], HOPS):
+    dq, dk, sem = refs[8:]
+    copies = []
+    for n, (ref, hop) in enumerate(zip(refs[:8], HOPS)):
         head = lax.rem(z - hop + RING, RING)
-        dq[:, pl.ds(pl.multiple_of(head * 2 * HEAD, 2 * HEAD), 2 * HEAD)] = ref[:, : 2 * HEAD]
-        dk[:, pl.ds(pl.multiple_of(head * HEAD, HEAD), HEAD)] = ref[:, 2 * HEAD :]
+        wide = pl.ds(pl.multiple_of(head * 2 * HEAD, 2 * HEAD), 2 * HEAD)
+        narrow = pl.ds(pl.multiple_of(head * HEAD, HEAD), HEAD)
+        copies.append(pltpu.make_async_copy(ref.at[:, pl.ds(0, 2 * HEAD)], dq.at[:, wide], sem.at[n]))
+        copies.append(pltpu.make_async_copy(ref.at[:, pl.ds(2 * HEAD, HEAD)], dk.at[:, narrow], sem.at[8 + n]))
+    for copy in copies:
+        copy.start()
+    for copy in copies:
+        copy.wait()
 
 
 def halves(w, core, part):
@@ -212,35 +237,38 @@
     return out
 
 
-def weight_kernel(hops, z_ref, features, *refs):
-    n = len(hops)
-    blocks, (gv, mine, other, lhs) = refs[:n], refs[n:]
-    z = z_ref[0]
-    part = features.shape[2]
-    for source in range(RING):
-        for row in range(2):
-            lhs[row * part : (row + 1) * part, 128 * source : 128 * source + 128] = features[source, row]
-    own = pl.ds(pl.multiple_of(z * 128, 128), 128)
-    for ref, hop in zip(blocks, hops):
-        head = lax.rem(z - hop + RING, RING)
-        gv[:, pl.ds(pl.multiple_of(head * HEAD, HEAD), HEAD)] = ref[own, :]
+def weight_kernel(n, z_ref, left, *refs):
+    blocks, (rows, mine, other) = refs[:n], refs[n : n + 3]
+    lhs = left
+    if len(refs) > n + 3:
+        lhs = refs[n + 3]
+        part = left.shape[2]
+        for source in range(RING):
+            for row in range(2):
+                lhs[row * part : (row + 1) * part, 128 * source : 128 * source + 128] = left[source, row]
+    part = lhs.shape[0] // 2
+    own = pl.ds(pl.multiple_of(z_ref[0] * 128, 128), 128)
+    for m, ref in enumerate(blocks):
+        rows[m] = ref[own, :]
         for row, (a, b) in enumerate(halves(nn(lhs[...], ref[...]), z_ref[1], part)):
-            mine[head, row] = a
-            other[head, row] = b
-
-
-def last_weight_kernel(z_ref, lhs, block, mine, other):
-    part = lhs.shape[0] // 2
-    for row, (a, b) in enumerate(halves(nn(lhs[...], block[...]), z_ref[1], part)):
-        mine[row] = a
-        other[row] = b
-
-
-def join_kernel(z_ref, both, last, got, out, total, sem):
-    total[...] = (last[...] + got[...].astype(F32)).astype(BF)
-    copy = pltpu.make_async_copy(total, out.at[lax.rem(z_ref[0] + 4, RING)], sem)
-    copy.start()
-    copy.wait()
+            mine[m, row] = a
+            other[m, row] = b
+
+
+def join_kernel(z_ref, *refs):
+    out = refs[-1]
+    for n, hops in enumerate(GROUPS):
+        for m, hop in enumerate(hops):
+            head = lax.rem(z_ref[0] - hop + RING, RING)
+            out[head] = (refs[2 * n][m] + refs[2 * n + 1][m].astype(F32)).astype(BF)
+
+
+def values_kernel(z_ref, *refs):
+    out = refs[-1]
+    for ref, hops in zip(refs[:-1], GROUPS):
+        for m, hop in enumerate(hops):
+            head = lax.rem(z_ref[0] - hop + RING, RING)
+            out[:, pl.ds(pl.multiple_of(head * HEAD, HEAD), HEAD)] = ref[m]
 
 
 def body(normed, queries, keys, values, out_grad, segment_ids):
@@ -256,7 +284,15 @@
     half = part // 2
     row = RING * count
 
-    packed = call(heads_kernel, shape(RING, count, 2 * HEAD), 2)(place, keys[0], values[0])
+    packed = pl.pallas_call(
+        heads_kernel,
+        out_shape=shape(RING, count, 2 * HEAD),
+        in_specs=[pl.BlockSpec(memory_space=pl.ANY)] * 2,
+        out_specs=VMEM,
+        scratch_shapes=[pltpu.SemaphoreType.DMA((2 * RING,))],
+        compiler_params=pltpu.CompilerParams(vmem_limit_bytes=60_000_000),
+        name="heads",
+    )(keys[0], values[0])
     kv_own = lax.all_to_all(packed, "z", 0, 0, tiled=True).reshape(row, 2 * HEAD)
     packed = call(pack_kernel, [shape(count, 4 * HEAD)] * 8, 2)(place, queries[0], out_grad[0])
     qg = [packed[0]]
@@ -272,8 +308,10 @@
         functools.partial(first_kernel, scale),
         [shape(row, HEAD), shape(row, HEAD, dtype=F32), shape(16, 256, dtype=F32), shape(row, 4 * HEAD)],
         11,
-        [pltpu.VMEM((2 * row, HEAD), F32), pltpu.VMEM((2 * row, HEAD), BF)],
+        [pltpu.VMEM((2 * row, HEAD), F32), pltpu.VMEM((2 * row, HEAD), BF), pltpu.SemaphoreType.DMA((RING,))],
         flops=2_000_000_000,
+        loose=range(1, 9),
+        limit=LARGE,
     )(place, lo, *qg, kv_own, kv_prev)
 
     got = lax.ppermute(dv_prev, "yl", [(1, 0)])
@@ -294,49 +332,43 @@
             5 + (n > 0),
             [pltpu.VMEM((2 * row, HEAD), BF), pltpu.VMEM((2 * row, HEAD), BF), pltpu.VMEM((HEAD, 2 * row), BF)],
             flops=1_500_000_000,
+            limit=LARGE,
         )(place, lo, rows, stats, kv_own, kv_prev, *([acc] if n else []))
         dq.append(piece)
     got = lax.ppermute(dk_prev, "yl", [(1, 0)])
-    back = call(functools.partial(back_kernel, softmax_scale), [shape(count, 3 * HEAD)] * 8, 4)(place, *dq, acc, got)
-    home = [back[0]]
+    pieces = {}
+    for hops in (SOON, LATE):
+        outs = call(
+            functools.partial(back_kernel, softmax_scale, hops), [shape(count, 3 * HEAD)] * len(hops), 4
+        )(place, *dq, acc, got)
+        pieces.update(zip(hops, outs))
+    home = [pieces[0]]
     for n in range(1, 8):
-        home.append(rotate(back[n], HOPS[n]))
+        home.append(rotate(pieces[HOPS[n]], HOPS[n]))
     grad_queries, grad_keys = call(
-        unpack_kernel, [shape(count, 2 * RING * HEAD), shape(count, RING * HEAD)], 8
+        unpack_kernel, [shape(count, 2 * RING * HEAD), shape(count, RING * HEAD)], 8,
+        [pltpu.SemaphoreType.DMA((16,))], loose=range(8),
     )(place, *home)
 
-    early = [h for h in HOPS if h != 4]
-    gv, mine, other, lhs = call(
-        functools.partial(weight_kernel, early),
-        [
-            shape(count, RING * HEAD),
-            shape(RING, 2, half, HEAD, dtype=F32),
-            shape(RING, 2, half, HEAD),
-            shape(2 * part, row),
-        ],
-        8,
-        flops=2_000_000_000,
-    )(place, spread, *[blocks[h] for h in early])
-    got = lax.ppermute(other, "core", [(0, 1), (1, 0)])
-    both = (mine + got.astype(F32)).astype(BF)
-    last, other = call(
-        last_weight_kernel, [shape(2, half, HEAD, dtype=F32), shape(2, half, HEAD)], 2, flops=300_000_000
-    )(place, lhs, blocks[4])
-    got = lax.ppermute(other, "core", [(0, 1), (1, 0)])
-    both = pl.pallas_call(
-        join_kernel,
-        out_shape=shape(RING, 2, half, HEAD),
-        in_specs=[SMEM, pl.BlockSpec(memory_space=pl.ANY), VMEM, VMEM],
-        out_specs=pl.BlockSpec(memory_space=pl.ANY),
-        scratch_shapes=[pltpu.VMEM((2, half, HEAD), BF), pltpu.SemaphoreType.DMA],
-        input_output_aliases={1: 0},
-        name="join",
-    )(place, both, last, got)
+    left = spread
+    values_own, sums = [], []
+    for n, hops in enumerate(GROUPS):
+        size = len(hops)
+        outs = [shape(size, count, HEAD), shape(size, 2, half, HEAD, dtype=F32), shape(size, 2, half, HEAD)]
+        if n == 0:
+            outs.append(shape(2 * part, row))
+        own_rows, mine, other, *lhs = call(
+            functools.partial(weight_kernel, size), outs, 1 + size, flops=300_000_000 * size
+        )(place, left, *[blocks[h] for h in hops])
+        if n == 0:
+            left = lhs[0]
+        values_own.append(own_rows)
+        sums += [mine, lax.ppermute(other, "core", [(0, 1), (1, 0)])]
+    both = call(join_kernel, shape(RING, 2, half, HEAD), 8)(place, *sums)
     arrived = lax.all_to_all(both.reshape(2 * RING, half, HEAD), ("x", "yh", "yl"), 0, 0, tiled=True)
     total = arrived.astype(F32).sum(axis=0) * (row * 2 * 16) ** (-0.5)
     grad_weight = jnp.concatenate([total[:, :64], total[:, 64:]], axis=0).astype(BF)
-    far = lax.dynamic_slice_in_dim(blocks[4], z * count, count, 0)
-    gv = lax.dynamic_update_slice_in_dim(gv, far, lax.rem(z + 4, RING) * HEAD, 1)
+    gv = call(values_kernel, shape(count, RING * HEAD), 4)(place, *values_own)
     return grad_queries[None], grad_keys[None], gv[None], grad_weight
 
 

time: 214 us -> 201 us (0.939)
  the two profiles are of different devices: /device:TPU:2 before, /device:TPU:120 now
where the time goes in v1:
time: 201 us; the launch traced here: 198 us
  waiting for transfers between devices  90.9 us (45%)
  starting transfers between devices  66.5 us (33%)
  Pallas kernels  33.5 us (17%)
  local copies, waits for them, and re-layouts  4.83 us (2%)
    ppermute x21, waiting for transfers between devices, rotate(): return lax.ppermute(x, 'z', [(i, (i + by) % RING) for i in range(RING)])  69.2 us
    ppermute x21, starting transfers between devices, rotate(): return lax.ppermute(x, 'z', [(i, (i + by) % RING) for i in range(RING)])  34.1 us
    all_to_all x1, waiting for transfers between devices, body(): lax.all_to_all(packed, 'z', 0, 0, tiled=True).reshape(row, 2 * HEAD)  11.4 us
    pallas_call x2, Pallas kernels, body(): call(functools.partial(second_kernel, scale, softmax_scale, lower, upper)...  9.72 us
    all_to_all x1, starting transfers between devices, body(): lax.all_to_all(both.reshape(2 * RING, half, HEAD), ('x', 'yh', 'yl'), 0,...  9.03 us
    all_to_all x1, starting transfers between devices, body(): lax.all_to_all(packed, 'z', 0, 0, tiled=True).reshape(row, 2 * HEAD)  7.67 us
    all_to_all x1, starting transfers between devices, body(): spread = lax.all_to_all(turned, 'z', 0, 0, tiled=True)  7.58 us
    pallas_call x4, Pallas kernels, body(): call(functools.partial(weight_kernel, size), outs, 1 + size, flops=300000...  6.83 us
  transfers between devices with their start and end apart: 31, of which 16 were waited for; matrix products, arithmetic and copies ran while one was open for 0% of the time, Pallas kernels for 15%

profile of v1, /device:TPU:120, one launch (start us, length us, event | category | flops | bytes accessed | tf_op | source)
XLA Modules:
  0.0 198.0 jit_solution(308124965802423752)
XLA Ops:
  0.7 2.0 %heads.1 = bf16[8,128,256]{2,1,0:T(8,128)(2,1)} custom-call(bf16[128,1024]{1,0:T(8,128)(2,1)} %bitcast.23, bf16[128,1024]{1,0:T(8,128)(2,1)} %bitcast.24), custom_call_target="tpu_custom_call" | custom-call | tf_op jit(solution)/shard_map/heads/pallas_call | solution.py:287
  2.7 7.7 %all-to-all-start = ((bf16[8,128,256]{2,1,0:T(8,128)(2,1)}), bf16[8,128,256]{2,1,0:T(8,128)(2,1)S(1)}, u32[]{:S(2)}, u32[]{:S(2)}) async-start(bf16[8,128,256]{2,1,0:T(8,128)(2,1)} %heads.1), calls=%async_computation | async-start | bytes 1048576 | tf_op jit(solution)/shard_map/all_to_all | solution.py:296
  10.5 2.1 %shard_map.93 = (bf16[8,2,336,128]{3,2,1,0:T(8,128)(2,1)}, s32[8,256]{1,0:T(8,128)S(1)}) custom-call(s32[3]{0:T(128)S(1)} %pad_add_fusion.z_ref, s32[16,128]{1,0:T(8,128)S(1)} %bitcast.21, bf16[128,5376]{1,0:T(8,128)(2,1)S(1)} %bitcast.14), custom_call_target="tpu_custom_call" | custom-call | flops 1000000 | bytes 2000000 | tf_op jit(solution)/shard_map/pallas_call | solution.py:301
  12.6 11.4 %all-to-all-done = bf16[8,128,256]{2,1,0:T(8,128)(2,1)S(1)} async-done(((bf16[8,128,256]{2,1,0:T(8,128)(2,1)}), bf16[8,128,256]{2,1,0:T(8,128)(2,1)S(1)}, u32[]{:S(2)}, u32[]{:S(2)}) %all-to-all-start) | async-done | bytes 524320 | tf_op jit(solution)/shard_map/all_to_all | solution.py:296
  23.9 7.6 %all-to-all-start.1 = ((bf16[8,2,336,128]{3,2,1,0:T(8,128)(2,1)}), bf16[8,2,336,128]{3,2,1,0:T(8,128)(2,1)S(1)}, u32[]{:S(2)}, u32[]{:S(2)}) async-start(bf16[8,2,336,128]{3,2,1,0:T(8,128)(2,1)} %get-tuple-element.72), calls=%async_computation.1 | async-start | bytes 2752512 | tf_op jit(solution)/shard_map/all_to_all | solution.py:305
  31.5 1.3 collective-permute-start.7
  32.8 0.7 shard_map.94
  33.5 2.8 %collective-permute-start = (bf16[128,512]{1,0:T(8,128)(2,1)S(1)}, bf16[128,512]{1,0:T(8,128)(2,1)S(1)}, u32[]{:S(2)}, u32[]{:S(2)}) collective-permute-start(bf16[128,512]{1,0:T(8,128)(2,1)S(1)} %get-tuple-element.48), channel_id=1, source_target_pairs={{0,4},{1,5},{2,6},{3,7},{4,0},{5,1},{6,2},{7,3},{8,12},{9,13},{10,... | collective-permute-start | bytes 393224 | tf_op jit(solution)/shard_map/ppermute | solution.py:49
  36.3 2.3 %collective-permute-start.1 = (bf16[128,512]{1,0:T(8,128)(2,1)S(1)}, bf16[128,512]{1,0:T(8,128)(2,1)S(1)}, u32[]{:S(2)}, u32[]{:S(2)}) collective-permute-start(bf16[128,512]{1,0:T(8,128)(2,1)S(1)} %get-tuple-element.49), channel_id=1, source_target_pairs={{0,3},{1,4},{2,5},{3,6},{4,7},{5,0},{6,1},{7,2},{8,11},{9,12},{10,... | collective-permute-start | bytes 393224 | tf_op jit(solution)/shard_map/ppermute | solution.py:49
  38.6 1.5 collective-permute-start.2
  40.1 2.6 %collective-permute-start.3 = (bf16[128,512]{1,0:T(8,128)(2,1)S(1)}, bf16[128,512]{1,0:T(8,128)(2,1)S(1)}, u32[]{:S(2)}, u32[]{:S(2)}) collective-permute-start(bf16[128,512]{1,0:T(8,128)(2,1)S(1)} %get-tuple-element.51), channel_id=1, source_target_pairs={{0,2},{1,3},{2,4},{3,5},{4,6},{5,7},{6,0},{7,1},{8,10},{9,11},{10,... | collective-permute-start | bytes 393224 | tf_op jit(solution)/shard_map/ppermute | solution.py:49
  42.8 31.8 %collective-permute-done.refs_1_ = bf16[128,512]{1,0:T(8,128)(2,1)S(1)} collective-permute-done((bf16[128,512]{1,0:T(8,128)(2,1)S(1)}, bf16[128,512]{1,0:T(8,128)(2,1)S(1)}, u32[]{:S(2)}, u32[]{:S(2)}) %collective-permute-start) | collective-permute-done | bytes 131104 | tf_op jit(solution)/shard_map/ppermute | solution.py:49
  74.5 3.9 %collective-permute-done.1.refs_2_ = bf16[128,512]{1,0:T(8,128)(2,1)S(1)} collective-permute-done((bf16[128,512]{1,0:T(8,128)(2,1)S(1)}, bf16[128,512]{1,0:T(8,128)(2,1)S(1)}, u32[]{:S(2)}, u32[]{:S(2)}) %collective-permute-start.1) | collective-permute-done | bytes 131104 | tf_op jit(solution)/shard_map/ppermute | solution.py:49
  78.4 2.5 %collective-permute-start.5 = (bf16[128,512]{1,0:T(8,128)(2,1)S(1)}, bf16[128,512]{1,0:T(8,128)(2,1)S(1)}, u32[]{:S(2)}, u32[]{:S(2)}) collective-permute-start(bf16[128,512]{1,0:T(8,128)(2,1)S(1)} %get-tuple-element.53), channel_id=1, source_target_pairs={{0,1},{1,2},{2,3},{3,4},{4,5},{5,6},{6,7},{7,0},{8,9},{9,10},{10,1... | collective-permute-start | bytes 393224 | tf_op jit(solution)/shard_map/ppermute | solution.py:49
  80.9 1.4 collective-permute-done.2.refs_3_
  82.2 1.5 collective-permute-done.4.refs_5_
  83.7 0.9 collective-permute-done.5.refs_6_
  84.6 3.8 %collective-permute-done.6.refs_7_ = bf16[128,512]{1,0:T(8,128)(2,1)S(1)} collective-permute-done((bf16[128,512]{1,0:T(8,128)(2,1)S(1)}, bf16[128,512]{1,0:T(8,128)(2,1)S(1)}, u32[]{:S(2)}, u32[]{:S(2)}) %collective-permute-start.6) | collective-permute-done | bytes 131104 | tf_op jit(solution)/shard_map/ppermute | solution.py:49
  88.4 6.2 %shard_map.95 = (bf16[1024,128]{1,0:T(8,128)(2,1)S(1)}, f32[1024,128]{1,0:T(8,128)S(1)}, f32[16,256]{1,0:T(8,128)S(1)}, bf16[1024,512]{1,0:T(8,128)(2,1)S(1)}) custom-call(s32[3]{0:T(128)S(1)} %pad_add_fusion.z_ref, s32[8,256]{1,0:T(8,128)S(1)} %get-tuple-element.46.lo_ref, bf16[128,512]{1,0:T(8,128)(2,1)S(1)} %get-tuple-element.47.refs_0_, ...), custom_call_target="tpu_custom_call" | custom-call | flops 2000000000 | bytes 2000000 | tf_op jit(solution)/shard_map/pallas_call | solution.py:307
  94.6 2.7 %collective-permute-start.16 = (bf16[1024,128]{1,0:T(8,128)(2,1)S(1)}, bf16[1024,128]{1,0:T(8,128)(2,1)S(1)}, u32[]{:S(2)}, u32[]{:S(2)}) collective-permute-start(bf16[1024,128]{1,0:T(8,128)(2,1)S(1)} %get-tuple-element.74), channel_id=1, source_target_pairs={{8,0},{9,1},{10,2},{11,3},{12,4},{13,5},{14,6},{15,7},{24,16},{25,... | collective-permute-start | bytes 786440 | tf_op jit(solution)/shard_map/ppermute | solution.py:317
  97.3 3.9 %collective-permute-done.16 = bf16[1024,128]{1,0:T(8,128)(2,1)S(1)} collective-permute-done((bf16[1024,128]{1,0:T(8,128)(2,1)S(1)}, bf16[1024,128]{1,0:T(8,128)(2,1)S(1)}, u32[]{:S(2)}, u32[]{:S(2)}) %collective-permute-start.16) | collective-permute-done | bytes 262176 | tf_op jit(solution)/shard_map/ppermute | solution.py:317
  101.3 0.2 collective-permute-start.17
  101.4 1.9 collective-permute-start.18
  103.4 4.8 %collective-permute-done.17.refs_1_ = bf16[1024,128]{1,0:T(8,128)(2,1)S(1)} collective-permute-done((bf16[1024,128]{1,0:T(8,128)(2,1)S(1)}, bf16[1024,128]{1,0:T(8,128)(2,1)S(1)}, u32[]{:S(2)}, u32[]{:S(2)}) %collective-permute-start.17) | collective-permute-done | bytes 262176 | tf_op jit(solution)/shard_map/ppermute | solution.py:49
  108.2 0.8 collective-permute-start.19
  109.0 0.7 copy-done.4
  109.7 1.2 collective-permute-start.20
  110.9 0.7 copy-done.8
  111.6 4.6 %collective-permute-done.19.refs_0_ = bf16[1024,128]{1,0:T(8,128)(2,1)S(1)} collective-permute-done((bf16[1024,128]{1,0:T(8,128)(2,1)S(1)}, bf16[1024,128]{1,0:T(8,128)(2,1)S(1)}, u32[]{:S(2)}, u32[]{:S(2)}) %collective-permute-start.19) | collective-permute-done | bytes 262176 | tf_op jit(solution)/shard_map/ppermute | solution.py:49
  116.2 1.3 collective-permute-start.21
  117.6 0.7 copy-done.6
  118.3 0.8 collective-permute-start.22
  119.1 5.9 %collective-permute-done.21.refs_0_ = bf16[1024,128]{1,0:T(8,128)(2,1)S(1)} collective-permute-done((bf16[1024,128]{1,0:T(8,128)(2,1)S(1)}, bf16[1024,128]{1,0:T(8,128)(2,1)S(1)}, u32[]{:S(2)}, u32[]{:S(2)}) %collective-permute-start.21) | collective-permute-done | bytes 262176 | tf_op jit(solution)/shard_map/ppermute | solution.py:49
  125.0 2.3 %collective-permute-start.23 = (bf16[1024,128]{1,0:T(8,128)(2,1)S(1)}, bf16[1024,128]{1,0:T(8,128)(2,1)S(1)}, u32[]{:S(2)}, u32[]{:S(2)}) collective-permute-start(bf16[1024,128]{1,0:T(8,128)(2,1)S(1)} %collective-permute-done.21.refs_0_), channel_id=1, source_target_pairs={{0,1},{1,2},{2,3},{3,4},{4,5},{5,6},{6,7},{7,0},{8,9},{9,10},{10,1... | collective-permute-start | bytes 786440 | tf_op jit(solution)/shard_map/ppermute | solution.py:49
  127.3 0.9 copy-done.5
  128.2 0.9 copy-done.9
  129.2 1.9 shard_map.101
  131.1 0.1 collective-permute-start.24
  131.2 1.9 shard_map.102
  133.1 0.6 collective-permute-start.25
  133.7 1.9 shard_map.103
  135.6 0.1 collective-permute-start.26
  135.7 1.1 shard_map.104
  136.8 0.6 collective-permute-start.27
  137.4 0.9 collective-permute-done.27.refs_7_
  138.3 1.6 shard_map.106
  139.9 9.0 %all-to-all-start.2 = ((bf16[16,168,128]{2,1,0:T(8,128)(2,1)}), bf16[16,168,128]{2,1,0:T(8,128)(2,1)}, u32[]{:S(2)}, u32[]{:S(2)}) async-start(bf16[16,168,128]{2,1,0:T(8,128)(2,1)} %bitcast.13), calls=%async_computation.2 | async-start | bytes 1376256 | tf_op jit(solution)/shard_map/all_to_all | solution.py:368
  148.9 4.9 %shard_map.96 = (f32[2048,128]{1,0:T(8,128)S(1)}, bf16[4,128,256]{2,1,0:T(8,128)(2,1)S(1)}, bf16[1024,128]{1,0:T(8,128)(2,1)}) custom-call(s32[3]{0:T(128)S(1)} %pad_add_fusion.z_ref, s32[8,256]{1,0:T(8,128)S(1)} %get-tuple-element.46.lo_ref, bf16[1024,512]{1,0:T(8,128)(2,1)S(1)} %copy-done.11, f32[16,256]{1,0:T(8,128)S(1)} %get-tuple-element.56.stats, ...), custom_call_target="tpu_custom_call" | custom-call | flops 1500000000 | bytes 2000000 | tf_op jit(solution)/shard_map/pallas_call | solution.py:329
  153.8 4.8 %shard_map.97 = (f32[2048,128]{1,0:T(8,128)S(1)}, bf16[4,128,256]{2,1,0:T(8,128)(2,1)S(1)}, bf16[1024,128]{1,0:T(8,128)(2,1)S(1)}) custom-call(s32[3]{0:T(128)S(1)} %pad_add_fusion.z_ref, s32[8,256]{1,0:T(8,128)S(1)} %get-tuple-element.46.lo_ref, bf16[1024,512]{1,0:T(8,128)(2,1)S(1)} %copy-done.11, f32[16,256]{1,0:T(8,128)S(1)} %get-tuple-element.56.stats, ...), custom_call_target="tpu_custom_call" | custom-call | flops 1500000000 | bytes 2000000 | tf_op jit(solution)/shard_map/pallas_call | solution.py:329
  158.6 2.8 %collective-permute-start.8 = (bf16[1024,128]{1,0:T(8,128)(2,1)S(1)}, bf16[1024,128]{1,0:T(8,128)(2,1)S(1)}, u32[]{:S(2)}, u32[]{:S(2)}) collective-permute-start(bf16[1024,128]{1,0:T(8,128)(2,1)S(1)} %get-tuple-element.61), channel_id=1, source_target_pairs={{8,0},{9,1},{10,2},{11,3},{12,4},{13,5},{14,6},{15,7},{24,16},{25,... | collective-permute-start | bytes 786440 | tf_op jit(solution)/shard_map/ppermute | solution.py:338
  161.4 5.5 %collective-permute-done.8.got = bf16[1024,128]{1,0:T(8,128)(2,1)S(1)} collective-permute-done((bf16[1024,128]{1,0:T(8,128)(2,1)S(1)}, bf16[1024,128]{1,0:T(8,128)(2,1)S(1)}, u32[]{:S(2)}, u32[]{:S(2)}) %collective-permute-start.8) | collective-permute-done | bytes 262176 | tf_op jit(solution)/shard_map/ppermute | solution.py:338
  166.9 0.6 shard_map.99
  167.6 1.5 collective-permute-start.10
  169.1 2.4 %collective-permute-start.11 = (bf16[128,384]{1,0:T(8,128)(2,1)S(1)}, bf16[128,384]{1,0:T(8,128)(2,1)S(1)}, u32[]{:S(2)}, u32[]{:S(2)}) collective-permute-start(bf16[128,384]{1,0:T(8,128)(2,1)S(1)} %get-tuple-element.65), channel_id=1, source_target_pairs={{0,5},{1,6},{2,7},{3,0},{4,1},{5,2},{6,3},{7,4},{8,13},{9,14},{10,... | collective-permute-start | bytes 294920 | tf_op jit(solution)/shard_map/ppermute | solution.py:49
  171.5 4.6 %collective-permute-start.9 = (bf16[128,384]{1,0:T(8,128)(2,1)S(1)}, bf16[128,384]{1,0:T(8,128)(2,1)S(1)}, u32[]{:S(2)}, u32[]{:S(2)}) collective-permute-start(bf16[128,384]{1,0:T(8,128)(2,1)S(1)} %get-tuple-element.63), channel_id=1, source_target_pairs={{0,4},{1,5},{2,6},{3,7},{4,0},{5,1},{6,2},{7,3},{8,12},{9,13},{10,... | collective-permute-start | bytes 294920 | tf_op jit(solution)/shard_map/ppermute | solution.py:49
  176.0 0.7 shard_map.98
  176.8 2.9 %collective-permute-start.13 = (bf16[128,384]{1,0:T(8,128)(2,1)S(1)}, bf16[128,384]{1,0:T(8,128)(2,1)S(1)}, u32[]{:S(2)}, u32[]{:S(2)}) collective-permute-start(bf16[128,384]{1,0:T(8,128)(2,1)S(1)} %get-tuple-element.67), channel_id=1, source_target_pairs={{0,6},{1,7},{2,0},{3,1},{4,2},{5,3},{6,4},{7,5},{8,14},{9,15},{10,... | collective-permute-start | bytes 294920 | tf_op jit(solution)/shard_map/ppermute | solution.py:49
  179.7 2.4 %collective-permute-start.14 = (bf16[128,384]{1,0:T(8,128)(2,1)S(1)}, bf16[128,384]{1,0:T(8,128)(2,1)S(1)}, u32[]{:S(2)}, u32[]{:S(2)}) collective-permute-start(bf16[128,384]{1,0:T(8,128)(2,1)S(1)} %get-tuple-element.68), channel_id=1, source_target_pairs={{0,1},{1,2},{2,3},{3,4},{4,5},{5,6},{6,7},{7,0},{8,9},{9,10},{10,1... | collective-permute-start | bytes 294920 | tf_op jit(solution)/shard_map/ppermute | solution.py:49
  182.1 4.9 %collective-permute-done.11.refs_3_ = bf16[128,384]{1,0:T(8,128)(2,1)S(1)} collective-permute-done((bf16[128,384]{1,0:T(8,128)(2,1)S(1)}, bf16[128,384]{1,0:T(8,128)(2,1)S(1)}, u32[]{:S(2)}, u32[]{:S(2)}) %collective-permute-start.11) | collective-permute-done | bytes 98336 | tf_op jit(solution)/shard_map/ppermute | solution.py:49
  187.1 5.8 %collective-permute-done.15.refs_7_ = bf16[128,384]{1,0:T(8,128)(2,1)S(1)} collective-permute-done((bf16[128,384]{1,0:T(8,128)(2,1)S(1)}, bf16[128,384]{1,0:T(8,128)(2,1)S(1)}, u32[]{:S(2)}, u32[]{:S(2)}) %collective-permute-start.15) | collective-permute-done | bytes 98336 | tf_op jit(solution)/shard_map/ppermute | solution.py:49
  192.9 1.7 shard_map.100
  194.6 1.3 shard_map.105
  196.0 1.2 convert_reduce_fusion
  197.3 0.7 copy.10
  (44 shorter events, 0.5 us)
Async XLA Ops:
  0.6 9.8 %copy-start.3 = (s32[1,2048]{1,0:T(1,128)S(1)}, s32[1,2048]{1,0:T(1,128)}, u32[]{:S(2)}) copy-start(s32[1,2048]{1,0:T(1,128)} %param.11) | copy-start | bytes 24580
  0.6 9.8 %copy-start = (bf16[1,128,5376]{2,1,0:T(8,128)(2,1)S(1)}, bf16[1,128,5376]{2,1,0:T(8,128)(2,1)}, u32[]{:S(2)}) copy-start(bf16[1,128,5376]{2,1,0:T(8,128)(2,1)} %param.6) | copy-start | bytes 4128772
  2.7 21.2 %all-to-all-start = ((bf16[8,128,256]{2,1,0:T(8,128)(2,1)}), bf16[8,128,256]{2,1,0:T(8,128)(2,1)S(1)}, u32[]{:S(2)}, u32[]{:S(2)}) async-start(bf16[8,128,256]{2,1,0:T(8,128)(2,1)} %heads.1), calls=%async_computation | async-start | bytes 1048576 | tf_op jit(solution)/shard_map/all_to_all | solution.py:296
  23.9 8.9 %copy-start.1 = (bf16[1,128,2048]{2,1,0:T(8,128)(2,1)S(1)}, bf16[1,128,2048]{2,1,0:T(8,128)(2,1)}, u32[]{:S(2)}) copy-start(bf16[1,128,2048]{2,1,0:T(8,128)(2,1)} %param.7) | copy-start | bytes 1572868
  23.9 8.9 %copy-start.2 = (bf16[1,128,2048]{2,1,0:T(8,128)(2,1)S(1)}, bf16[1,128,2048]{2,1,0:T(8,128)(2,1)}, u32[]{:S(2)}) copy-start(bf16[1,128,2048]{2,1,0:T(8,128)(2,1)} %param.10) | copy-start | bytes 1572868
  23.9 103.3 %all-to-all-start.1 = ((bf16[8,2,336,128]{3,2,1,0:T(8,128)(2,1)}), bf16[8,2,336,128]{3,2,1,0:T(8,128)(2,1)S(1)}, u32[]{:S(2)}, u32[]{:S(2)}) async-start(bf16[8,2,336,128]{3,2,1,0:T(8,128)(2,1)} %get-tuple-element.72), calls=%async_computation.1 | async-start | bytes 2752512 | tf_op jit(solution)/shard_map/all_to_all | solution.py:305
  31.5 56.9 %collective-permute-start.7 = (bf16[1024,256]{1,0:T(8,128)(2,1)S(1)}, bf16[1024,256]{1,0:T(8,128)(2,1)S(1)}, u32[]{:S(2)}, u32[]{:S(2)}) collective-permute-start(bf16[1024,256]{1,0:T(8,128)(2,1)S(1)} %bitcast.15), channel_id=1, source_target_pairs={{0,8},{1,9},{2,10},{3,11},{4,12},{5,13},{6,14},{7,15},{16,24},{17,... | collective-permute-start | bytes 1572872 | tf_op jit(solution)/shard_map/ppermute | solution.py:304
  33.5 41.0 %collective-permute-start = (bf16[128,512]{1,0:T(8,128)(2,1)S(1)}, bf16[128,512]{1,0:T(8,128)(2,1)S(1)}, u32[]{:S(2)}, u32[]{:S(2)}) collective-permute-start(bf16[128,512]{1,0:T(8,128)(2,1)S(1)} %get-tuple-element.48), channel_id=1, source_target_pairs={{0,4},{1,5},{2,6},{3,7},{4,0},{5,1},{6,2},{7,3},{8,12},{9,13},{10,... | collective-permute-start | bytes 393224 | tf_op jit(solution)/shard_map/ppermute | solution.py:49
  36.3 42.1 %collective-permute-start.1 = (bf16[128,512]{1,0:T(8,128)(2,1)S(1)}, bf16[128,512]{1,0:T(8,128)(2,1)S(1)}, u32[]{:S(2)}, u32[]{:S(2)}) collective-permute-start(bf16[128,512]{1,0:T(8,128)(2,1)S(1)} %get-tuple-element.49), channel_id=1, source_target_pairs={{0,3},{1,4},{2,5},{3,6},{4,7},{5,0},{6,1},{7,2},{8,11},{9,12},{10,... | collective-permute-start | bytes 393224 | tf_op jit(solution)/shard_map/ppermute | solution.py:49
  38.6 43.6 %collective-permute-start.2 = (bf16[128,512]{1,0:T(8,128)(2,1)S(1)}, bf16[128,512]{1,0:T(8,128)(2,1)S(1)}, u32[]{:S(2)}, u32[]{:S(2)}) collective-permute-start(bf16[128,512]{1,0:T(8,128)(2,1)S(1)} %get-tuple-element.50), channel_id=1, source_target_pairs={{0,5},{1,6},{2,7},{3,0},{4,1},{5,2},{6,3},{7,4},{8,13},{9,14},{10,... | collective-permute-start | bytes 393224 | tf_op jit(solution)/shard_map/ppermute | solution.py:49
  40.1 42.1 %collective-permute-start.3 = (bf16[128,512]{1,0:T(8,128)(2,1)S(1)}, bf16[128,512]{1,0:T(8,128)(2,1)S(1)}, u32[]{:S(2)}, u32[]{:S(2)}) collective-permute-start(bf16[128,512]{1,0:T(8,128)(2,1)S(1)} %get-tuple-element.51), channel_id=1, source_target_pairs={{0,2},{1,3},{2,4},{3,5},{4,6},{5,7},{6,0},{7,1},{8,10},{9,11},{10,... | collective-permute-start | bytes 393224 | tf_op jit(solution)/shard_map/ppermute | solution.py:49
  74.5 9.2 %collective-permute-start.4 = (bf16[128,512]{1,0:T(8,128)(2,1)S(1)}, bf16[128,512]{1,0:T(8,128)(2,1)S(1)}, u32[]{:S(2)}, u32[]{:S(2)}) collective-permute-start(bf16[128,512]{1,0:T(8,128)(2,1)S(1)} %get-tuple-element.52), channel_id=1, source_target_pairs={{0,6},{1,7},{2,0},{3,1},{4,2},{5,3},{6,4},{7,5},{8,14},{9,15},{10,... | collective-permute-start | bytes 393224 | tf_op jit(solution)/shard_map/ppermute | solution.py:49
  78.4 6.3 %collective-permute-start.5 = (bf16[128,512]{1,0:T(8,128)(2,1)S(1)}, bf16[128,512]{1,0:T(8,128)(2,1)S(1)}, u32[]{:S(2)}, u32[]{:S(2)}) collective-permute-start(bf16[128,512]{1,0:T(8,128)(2,1)S(1)} %get-tuple-element.53), channel_id=1, source_target_pairs={{0,1},{1,2},{2,3},{3,4},{4,5},{5,6},{6,7},{7,0},{8,9},{9,10},{10,1... | collective-permute-start | bytes 393224 | tf_op jit(solution)/shard_map/ppermute | solution.py:49
  82.2 6.2 %collective-permute-start.6 = (bf16[128,512]{1,0:T(8,128)(2,1)S(1)}, bf16[128,512]{1,0:T(8,128)(2,1)S(1)}, u32[]{:S(2)}, u32[]{:S(2)}) collective-permute-start(bf16[128,512]{1,0:T(8,128)(2,1)S(1)} %get-tuple-element.54), channel_id=1, source_target_pairs={{0,7},{1,0},{2,1},{3,2},{4,3},{5,4},{6,5},{7,6},{8,15},{9,8},{10,9... | collective-permute-start | bytes 393224 | tf_op jit(solution)/shard_map/ppermute | solution.py:49
  94.6 30.3 %copy-start.10 = (bf16[1024,512]{1,0:T(8,128)(2,1)}, bf16[1024,512]{1,0:T(8,128)(2,1)S(1)}, u32[]{:S(2)}) copy-start(bf16[1024,512]{1,0:T(8,128)(2,1)S(1)} %get-tuple-element.55.qg) | copy-start | bytes 3145732
  94.6 6.5 %collective-permute-start.16 = (bf16[1024,128]{1,0:T(8,128)(2,1)S(1)}, bf16[1024,128]{1,0:T(8,128)(2,1)S(1)}, u32[]{:S(2)}, u32[]{:S(2)}) collective-permute-start(bf16[1024,128]{1,0:T(8,128)(2,1)S(1)} %get-tuple-element.74), channel_id=1, source_target_pairs={{8,0},{9,1},{10,2},{11,3},{12,4},{13,5},{14,6},{15,7},{24,16},{25,... | collective-permute-start | bytes 786440 | tf_op jit(solution)/shard_map/ppermute | solution.py:317
  101.3 6.9 %collective-permute-start.17 = (bf16[1024,128]{1,0:T(8,128)(2,1)S(1)}, bf16[1024,128]{1,0:T(8,128)(2,1)S(1)}, u32[]{:S(2)}, u32[]{:S(2)}) collective-permute-start(bf16[1024,128]{1,0:T(8,128)(2,1)S(1)} %add_convert_fusion.refs_0_), channel_id=1, source_target_pairs={{0,1},{1,2},{2,3},{3,4},{4,5},{5,6},{6,7},{7,0},{8,9},{9,10},{10,1... | collective-permute-start | bytes 786440 | tf_op jit(solution)/shard_map/ppermute | solution.py:49
  101.4 8.3 %collective-permute-start.18 = (bf16[1024,128]{1,0:T(8,128)(2,1)S(1)}, bf16[1024,128]{1,0:T(8,128)(2,1)S(1)}, u32[]{:S(2)}, u32[]{:S(2)}) collective-permute-start(bf16[1024,128]{1,0:T(8,128)(2,1)S(1)} %add_convert_fusion.refs_0_), channel_id=1, source_target_pairs={{0,7},{1,0},{2,1},{3,2},{4,3},{5,4},{6,5},{7,6},{8,15},{9,8},{10,9... | collective-permute-start | bytes 786440 | tf_op jit(solution)/shard_map/ppermute | solution.py:49
  108.2 8.0 %collective-permute-start.19 = (bf16[1024,128]{1,0:T(8,128)(2,1)S(1)}, bf16[1024,128]{1,0:T(8,128)(2,1)S(1)}, u32[]{:S(2)}, u32[]{:S(2)}) collective-permute-start(bf16[1024,128]{1,0:T(8,128)(2,1)S(1)} %collective-permute-done.17.refs_1_), channel_id=1, source_target_pairs={{0,1},{1,2},{2,3},{3,4},{4,5},{5,6},{6,7},{7,0},{8,9},{9,10},{10,1... | collective-permute-start | bytes 786440 | tf_op jit(solution)/shard_map/ppermute | solution.py:49
  109.0 0.7 copy-start.4
  109.7 8.6 %collective-permute-start.20 = (bf16[1024,128]{1,0:T(8,128)(2,1)S(1)}, bf16[1024,128]{1,0:T(8,128)(2,1)}, u32[]{:S(2)}, u32[]{:S(2)}) collective-permute-start(bf16[1024,128]{1,0:T(8,128)(2,1)S(1)} %collective-permute-done.18.refs_2_), channel_id=1, source_target_pairs={{0,7},{1,0},{2,1},{3,2},{4,3},{5,4},{6,5},{7,6},{8,15},{9,8},{10,9... | collective-permute-start | bytes 786440 | tf_op jit(solution)/shard_map/ppermute | solution.py:49
  110.9 0.7 copy-start.8
  116.2 8.8 %collective-permute-start.21 = (bf16[1024,128]{1,0:T(8,128)(2,1)S(1)}, bf16[1024,128]{1,0:T(8,128)(2,1)S(1)}, u32[]{:S(2)}, u32[]{:S(2)}) collective-permute-start(bf16[1024,128]{1,0:T(8,128)(2,1)S(1)} %collective-permute-done.19.refs_0_), channel_id=1, source_target_pairs={{0,1},{1,2},{2,3},{3,4},{4,5},{5,6},{6,7},{7,0},{8,9},{9,10},{10,1... | collective-permute-start | bytes 786440 | tf_op jit(solution)/shard_map/ppermute | solution.py:49
  117.6 0.7 copy-start.6
  118.3 15.3 %collective-permute-start.22 = (bf16[1024,128]{1,0:T(8,128)(2,1)}, bf16[1024,128]{1,0:T(8,128)(2,1)}, u32[]{:S(2)}, u32[]{:S(2)}) collective-permute-start(bf16[1024,128]{1,0:T(8,128)(2,1)} %collective-permute-done.20.refs_1_), channel_id=1, source_target_pairs={{0,7},{1,0},{2,1},{3,2},{4,3},{5,4},{6,5},{7,6},{8,15},{9,8},{10,9... | collective-permute-start | bytes 786440 | tf_op jit(solution)/shard_map/ppermute | solution.py:49
  125.0 10.7 %collective-permute-start.23 = (bf16[1024,128]{1,0:T(8,128)(2,1)S(1)}, bf16[1024,128]{1,0:T(8,128)(2,1)S(1)}, u32[]{:S(2)}, u32[]{:S(2)}) collective-permute-start(bf16[1024,128]{1,0:T(8,128)(2,1)S(1)} %collective-permute-done.21.refs_0_), channel_id=1, source_target_pairs={{0,1},{1,2},{2,3},{3,4},{4,5},{5,6},{6,7},{7,0},{8,9},{9,10},{10,1... | collective-permute-start | bytes 786440 | tf_op jit(solution)/shard_map/ppermute | solution.py:49
  127.2 1.0 copy-start.5
  128.2 0.9 copy-start.9
  129.2 2.0 %copy-start.7 = (bf16[1024,128]{1,0:T(8,128)(2,1)S(1)}, bf16[1024,128]{1,0:T(8,128)(2,1)}, u32[]{:S(2)}) copy-start(bf16[1024,128]{1,0:T(8,128)(2,1)} %copy-done.6) | copy-start | bytes 786436
  131.1 6.3 %collective-permute-start.24 = (bf16[3,2,168,128]{3,2,1,0:T(8,128)(2,1)S(1)}, bf16[3,2,168,128]{3,2,1,0:T(8,128)(2,1)S(1)}, u32[]{:S(2)}, u32[]{:S(2)}) collective-permute-start(bf16[3,2,168,128]{3,2,1,0:T(8,128)(2,1)S(1)} %get-tuple-element.81), channel_id=1, source_target_pairs={{0,16},{16,0},{1,17},{17,1},{2,18},{18,2},{3,19},{19,3},{4,20},{20... | collective-permute-start | bytes 774152 | tf_op jit(solution)/shard_map/ppermute | solution.py:366
  133.1 4.3 %collective-permute-start.25 = (bf16[2,2,168,128]{3,2,1,0:T(8,128)(2,1)S(1)}, bf16[2,2,168,128]{3,2,1,0:T(8,128)(2,1)S(1)}, u32[]{:S(2)}, u32[]{:S(2)}) collective-permute-start(bf16[2,2,168,128]{3,2,1,0:T(8,128)(2,1)S(1)} %get-tuple-element.83), channel_id=1, source_target_pairs={{0,16},{16,0},{1,17},{17,1},{2,18},{18,2},{3,19},{19,3},{4,20},{20... | collective-permute-start | bytes 516104 | tf_op jit(solution)/shard_map/ppermute | solution.py:366
  135.6 1.8 collective-permute-start.26
  136.8 1.5 collective-permute-start.27
  139.9 9.0 %copy-start.11 = (bf16[1024,512]{1,0:T(8,128)(2,1)S(1)}, bf16[1024,512]{1,0:T(8,128)(2,1)}, u32[]{:S(2)}) copy-start(bf16[1024,512]{1,0:T(8,128)(2,1)} %copy-done.10) | copy-start | bytes 3145732
  139.9 56.1 %all-to-all-start.2 = ((bf16[16,168,128]{2,1,0:T(8,128)(2,1)}), bf16[16,168,128]{2,1,0:T(8,128)(2,1)}, u32[]{:S(2)}, u32[]{:S(2)}) async-start(bf16[16,168,128]{2,1,0:T(8,128)(2,1)} %bitcast.13), calls=%async_computation.2 | async-start | bytes 1376256 | tf_op jit(solution)/shard_map/all_to_all | solution.py:368
  158.6 8.3 %collective-permute-start.8 = (bf16[1024,128]{1,0:T(8,128)(2,1)S(1)}, bf16[1024,128]{1,0:T(8,128)(2,1)S(1)}, u32[]{:S(2)}, u32[]{:S(2)}) collective-permute-start(bf16[1024,128]{1,0:T(8,128)(2,1)S(1)} %get-tuple-element.61), channel_id=1, source_target_pairs={{8,0},{9,1},{10,2},{11,3},{12,4},{13,5},{14,6},{15,7},{24,16},{25,... | collective-permute-start | bytes 786440 | tf_op jit(solution)/shard_map/ppermute | solution.py:338
  167.6 12.1 %collective-permute-start.10 = (bf16[128,384]{1,0:T(8,128)(2,1)S(1)}, bf16[128,384]{1,0:T(8,128)(2,1)S(1)}, u32[]{:S(2)}, u32[]{:S(2)}) collective-permute-start(bf16[128,384]{1,0:T(8,128)(2,1)S(1)} %get-tuple-element.64), channel_id=1, source_target_pairs={{0,3},{1,4},{2,5},{3,6},{4,7},{5,0},{6,1},{7,2},{8,11},{9,12},{10,... | collective-permute-start | bytes 294920 | tf_op jit(solution)/shard_map/ppermute | solution.py:49
  169.1 18.0 %collective-permute-start.11 = (bf16[128,384]{1,0:T(8,128)(2,1)S(1)}, bf16[128,384]{1,0:T(8,128)(2,1)S(1)}, u32[]{:S(2)}, u32[]{:S(2)}) collective-permute-start(bf16[128,384]{1,0:T(8,128)(2,1)S(1)} %get-tuple-element.65), channel_id=1, source_target_pairs={{0,5},{1,6},{2,7},{3,0},{4,1},{5,2},{6,3},{7,4},{8,13},{9,14},{10,... | collective-permute-start | bytes 294920 | tf_op jit(solution)/shard_map/ppermute | solution.py:49
  171.5 15.6 %collective-permute-start.9 = (bf16[128,384]{1,0:T(8,128)(2,1)S(1)}, bf16[128,384]{1,0:T(8,128)(2,1)S(1)}, u32[]{:S(2)}, u32[]{:S(2)}) collective-permute-start(bf16[128,384]{1,0:T(8,128)(2,1)S(1)} %get-tuple-element.63), channel_id=1, source_target_pairs={{0,4},{1,5},{2,6},{3,7},{4,0},{5,1},{6,2},{7,3},{8,12},{9,13},{10,... | collective-permute-start | bytes 294920 | tf_op jit(solution)/shard_map/ppermute | solution.py:49
  176.7 10.4 %collective-permute-start.12 = (bf16[128,384]{1,0:T(8,128)(2,1)S(1)}, bf16[128,384]{1,0:T(8,128)(2,1)S(1)}, u32[]{:S(2)}, u32[]{:S(2)}) collective-permute-start(bf16[128,384]{1,0:T(8,128)(2,1)S(1)} %get-tuple-element.66), channel_id=1, source_target_pairs={{0,2},{1,3},{2,4},{3,5},{4,6},{5,7},{6,0},{7,1},{8,10},{9,11},{10,... | collective-permute-start | bytes 294920 | tf_op jit(solution)/shard_map/ppermute | solution.py:49
  176.8 10.3 %collective-permute-start.13 = (bf16[128,384]{1,0:T(8,128)(2,1)S(1)}, bf16[128,384]{1,0:T(8,128)(2,1)S(1)}, u32[]{:S(2)}, u32[]{:S(2)}) collective-permute-start(bf16[128,384]{1,0:T(8,128)(2,1)S(1)} %get-tuple-element.67), channel_id=1, source_target_pairs={{0,6},{1,7},{2,0},{3,1},{4,2},{5,3},{6,4},{7,5},{8,14},{9,15},{10,... | collective-permute-start | bytes 294920 | tf_op jit(solution)/shard_map/ppermute | solution.py:49
  179.7 7.4 %collective-permute-start.14 = (bf16[128,384]{1,0:T(8,128)(2,1)S(1)}, bf16[128,384]{1,0:T(8,128)(2,1)S(1)}, u32[]{:S(2)}, u32[]{:S(2)}) collective-permute-start(bf16[128,384]{1,0:T(8,128)(2,1)S(1)} %get-tuple-element.68), channel_id=1, source_target_pairs={{0,1},{1,2},{2,3},{3,4},{4,5},{5,6},{6,7},{7,0},{8,9},{9,10},{10,1... | collective-permute-start | bytes 294920 | tf_op jit(solution)/shard_map/ppermute | solution.py:49
  187.1 5.8 %collective-permute-start.15 = (bf16[128,384]{1,0:T(8,128)(2,1)S(1)}, bf16[128,384]{1,0:T(8,128)(2,1)S(1)}, u32[]{:S(2)}, u32[]{:S(2)}) collective-permute-start(bf16[128,384]{1,0:T(8,128)(2,1)S(1)} %get-tuple-element.69), channel_id=1, source_target_pairs={{0,7},{1,0},{2,1},{3,2},{4,3},{5,4},{6,5},{7,6},{8,15},{9,8},{10,9... | collective-permute-start | bytes 294920 | tf_op jit(solution)/shard_map/ppermute | solution.py:49
